TPU v7x, 128 devices: a whole 4x4x4 slice. The times are simulated.
128 devices in a mesh: dp: 4 (over x), expert: 32 (over z, y, core).
Axes of the slice: x: 4, y: 4, z: 4, core: 2. Of those that a mesh axis runs over, the one named last changes fastest.
Arguments:
- tokens: bfloat16 [32, 512, 4096], P('expert', 'dp'), may hold values from -6 to 6
- w_gate: bfloat16 [32, 4096, 896], P('expert'), may hold values from -0.09375 to 0.09375
- w_up: bfloat16 [32, 4096, 896], P('expert'), may hold values from -0.09375 to 0.09375
- w_down: bfloat16 [32, 896, 4096], P('expert'), may hold values from -0.1875 to 0.1875
- expert_ids: int32 [32, 512, 4], P('expert'), may hold values from 0 to 31, all different within a row
- gate_index: int32 [32, 512, 4], P('expert'), may hold values from 0 to 255
- gate_table: float32 [256], replicated, may hold values from 0.05 to 1
- spill: int32 [32, 512], P('expert'), may hold values from 0 to 3, as said below
Outputs:
- mixed: bfloat16 [32, 512, 4096], P('expert', 'dp')
Inputs may be any that keep to these rules, and one draw needn't show every extreme that they name: `spill`: A token is dispatched by a device of its own column. Of the 128 tokens of one device at most 32 are dispatched by any one other device, and in every draw some device hands exactly 32 to some peer.
All inputs are finite; a program needn't handle non-finite values.
Results may differ from a plain program's by a relative error of at most 0.0058.
Values may be sent and summed in bfloat16 or wider, within the bound.
No kernel may reach another device: no remote copies, remote signals or barrier semaphores. Data moves between devices by JAX's collectives and lax.ppermute only.
A program may use at most 128 MiB of HBM per device.

v0:
```python
import functools
import jax
import jax.numpy as jnp
from jax import lax
from jax.experimental import pallas as pl
from jax.experimental.pallas import tpu as pltpu
from jax.sharding import PartitionSpec as P

F32 = jnp.float32
BF16 = jnp.bfloat16
I32 = jnp.int32


def onehot(mask):
    return jnp.where(mask, 1.0, 0.0).astype(BF16)


def strict_upper(n):
    return onehot(lax.broadcasted_iota(I32, (n, n), 0) < lax.broadcasted_iota(I32, (n, n), 1))


def dot(a, b):
    return jnp.dot(a, b, preferred_element_type=F32)


def dot_nt(a, b):
    return lax.dot_general(a, b, (((1,), (1,)), ((), ())), preferred_element_type=F32)


def dot_tn(a, b):
    return lax.dot_general(a, b, (((0,), (0,)), ((), ())), preferred_element_type=F32)


def send(buf_ref, out_ref, sems, j):
    return pltpu.make_async_copy(buf_ref, out_ref, sems.at[j])


def parts(width, count):
    step = width // count
    return [pl.ds(j * step, step) for j in range(count)]


PIECES = 4


def spill_kernel(dp_count, room, me_ref, spill_ref, tok_ref, pick_ref, own_ref, *refs):
    out_refs, (spill_buf, buf, spill_sem, in_sems, out_sems) = refs[: dp_count - 1], refs[dp_count - 1 :]
    own_rows, width = tok_ref.shape
    slots = pick_ref.shape[0]
    load = pltpu.make_async_copy(spill_ref, spill_buf, spill_sem)
    load.start()
    cols = parts(width, PIECES)
    loads = [send(tok_ref.at[:, c], own_ref.at[:, c], in_sems, j) for j, c in enumerate(cols)]
    for copy in loads:
        copy.start()
    load.wait()
    me = me_ref[0]
    senders = spill_buf[pl.ds(me, 1), :]
    peers = lax.broadcasted_iota(I32, (8, own_rows), 0)
    same = onehot(senders == peers)
    before = dot(same, strict_upper(own_rows))
    order = jnp.sum(before * same.astype(F32), axis=0, keepdims=True).astype(I32)
    ahead = jnp.where(senders < me, senders - me + dp_count, senders - me)
    target = jnp.where(ahead == 0, slots, (ahead - 1) * room + order)
    rows = lax.broadcasted_iota(I32, (slots, own_rows), 0)
    pick = onehot(rows == target)
    pick_ref[...] = pick
    stores = []
    for j, c in enumerate(cols):
        loads[j].wait()
        buf[:, c] = dot(pick, own_ref[:, c]).astype(BF16)
        for k, out_ref in enumerate(out_refs):
            store = send(buf.at[pl.ds(k * room, room), c], out_ref.at[:, c], out_sems, j * len(out_refs) + k)
            store.start()
            stores.append(store)
    for store in stores:
        store.wait()


Z, Y, C = 4, 4, 2


def partner(me, k, sign):
    z = (me // (Y * C) + sign * (k // (Y * C))) % Z
    y = (me // C % Y + sign * (k // C % Y)) % Y
    c = (me % C + k % C) % C
    return (z * Y + y) * C + c


def slot_of(index, experts_all, capacity, first):
    cut = experts_all * first
    in_first = index < cut
    expert = jnp.where(in_first, index // first, (index - cut) // (capacity - first))
    rank = jnp.where(in_first, index % first, first + (index - cut) % (capacity - first))
    return expert, rank + 1


def route_kernel(
    dp_count, room, experts_all, capacity, first, me_ref, spill_ref, ids_ref, weight_ref,
    pick_ref, own_w_ref, arr_w_ref
):
    me = me_ref[0]
    own_rows = spill_ref.shape[1]
    top_count, column_tokens = ids_ref.shape
    source_rows = own_rows + (dp_count - 1) * room
    slots = experts_all * capacity

    by_home = onehot(spill_ref[...] == me)
    order = dot(by_home, strict_upper(own_rows)).astype(I32)
    homes = lax.broadcasted_iota(I32, (dp_count, own_rows), 0)
    place = lax.broadcasted_iota(I32, (dp_count, own_rows), 1)
    back = jnp.where(homes > me, me - homes + dp_count, me - homes)
    row = jnp.where(back == 0, place, own_rows + (back - 1) * room + order)
    row = jnp.where(spill_ref[...] == me, row, source_rows)
    row = jnp.concatenate([row[h : h + 1] for h in range(dp_count)], axis=1)
    to_row = onehot(lax.broadcasted_iota(I32, (source_rows, column_tokens), 0) == row)

    experts = lax.broadcasted_iota(I32, (experts_all, column_tokens), 0)
    scale = jnp.zeros((experts_all, column_tokens), F32)
    chosen = jnp.zeros((experts_all, column_tokens), F32)
    mine = row < source_rows
    for k in range(top_count):
        hit = (ids_ref[k : k + 1, :] == experts) & mine
        scale = jnp.where(hit, weight_ref[k : k + 1, :], scale)
        chosen = jnp.where(hit, 1.0, chosen)
    rank = dot(chosen.astype(BF16), strict_upper(column_tokens))
    keep = (chosen > 0.0) & (rank < capacity)
    code = jnp.where(keep, rank + 1.0, 0.0).astype(BF16)
    scale = jnp.where(keep, scale, 0.0)
    high = scale.astype(BF16)
    low = (scale - high.astype(F32)).astype(BF16)

    slot_expert, _ = slot_of(lax.broadcasted_iota(I32, (slots, experts_all), 0), experts_all, capacity, first)
    slot_row = lax.broadcasted_iota(I32, (slots, experts_all), 0)
    slot_expert = jnp.where(slot_row < experts_all * first, slot_expert, partner(me_ref[1], slot_expert, 1))
    spread = onehot(slot_expert == lax.broadcasted_iota(I32, (slots, experts_all), 1))
    code_rows = dot_nt(code, to_row).astype(BF16)
    _, rank_col = slot_of(lax.broadcasted_iota(I32, (slots, source_rows), 0), experts_all, capacity, first)
    pick_ref[...] = onehot(dot(spread, code_rows).astype(I32) == rank_col)

    slot_expert, _ = slot_of(lax.broadcasted_iota(I32, (experts_all, slots), 1), experts_all, capacity, first)
    spread_t = onehot(slot_expert == lax.broadcasted_iota(I32, (experts_all, slots), 0))
    _, rank_row = slot_of(lax.broadcasted_iota(I32, (source_rows, slots), 1), experts_all, capacity, first)
    code_t = dot_nt(to_row, code).astype(BF16)
    filled = dot(code_t, spread_t).astype(I32) == rank_row
    high_t = dot(dot_nt(to_row, high).astype(BF16), spread_t)
    low_t = dot(dot_nt(to_row, low).astype(BF16), spread_t)
    high_w = jnp.where(filled, high_t, 0.0).astype(BF16)
    low_w = jnp.where(filled, low_t, 0.0).astype(BF16)
    own_w_ref[:own_rows] = high_w[:own_rows]
    own_w_ref[own_rows:] = low_w[:own_rows]
    arr_w_ref[: source_rows - own_rows] = high_w[own_rows:]
    arr_w_ref[source_rows - own_rows :] = low_w[own_rows:]


def build_kernel(pick_ref, *refs):
    *src_refs, out_ref, buf, sems = refs
    copies = []
    for j, c in enumerate(parts(out_ref.shape[1], PIECES)):
        rows = jnp.concatenate([ref[:, c] for ref in src_refs], axis=0)
        buf[:, c] = dot(pick_ref[...], rows).astype(BF16)
        copies.append(send(buf.at[:, c], out_ref.at[:, c], sems, j))
        copies[-1].start()
    for copy in copies:
        copy.wait()


def build_blocks_kernel(size, pick_ref, *refs):
    count = pick_ref.shape[0] // size
    src_refs, out_refs, (buf, sems) = refs[: -count - 2], refs[-count - 2 : -2], refs[-2:]
    for c in parts(buf.shape[1], PIECES):
        rows = jnp.concatenate([ref[:, c] for ref in src_refs], axis=0)
        buf[:, c] = dot(pick_ref[...], rows).astype(BF16)
    copies = [send(buf.at[pl.ds(k * size, size)], out_ref, sems, k) for k, out_ref in enumerate(out_refs)]
    for copy in copies:
        copy.start()
    for copy in copies:
        copy.wait()


GATE_COLS = 128
DOWN_COLS = 1024


def ffn_kernel(blocks, me_ref, *refs):
    x_in, (gate_in, up_in, down_in, out_ref, x, both, down, acc, hidden, buf) = refs[:blocks], refs[blocks : blocks + 10]
    x_sem, top_sem, both_sem, down_sem, out_sem = refs[blocks + 10 :]
    depth = x.shape[1] // PIECES
    tiles, downs = both.shape[0], down.shape[0]
    size = x.shape[0] // blocks

    def lanes(n, step):
        return pl.ds(pl.multiple_of(n * step, step), step)

    def fetch(n):
        cols = lanes(n, GATE_COLS)
        return (
            pltpu.make_async_copy(gate_in.at[:, cols], both.at[n, :, pl.ds(0, GATE_COLS)], both_sem.at[n, 0]),
            pltpu.make_async_copy(up_in.at[:, cols], both.at[n, :, pl.ds(GATE_COLS, GATE_COLS)], both_sem.at[n, 1]),
        )

    def fetch_down(n):
        return pltpu.make_async_copy(down_in.at[:, lanes(n, DOWN_COLS)], down.at[n], down_sem.at[n])

    def store(n):
        cols = lanes(n, DOWN_COLS)
        return pltpu.make_async_copy(buf.at[:, cols], out_ref.at[:, cols], out_sem.at[n])

    def activate(n):
        gate_part, up_part = acc[:, :GATE_COLS], acc[:, GATE_COLS:]
        hidden[:, lanes(n, GATE_COLS)] = (jax.nn.silu(gate_part) * up_part).astype(BF16)

    def top(k):
        d = lanes(k, depth)
        rows = [] if blocks > 1 else [pltpu.make_async_copy(x_in[0].at[:, d], x.at[:, d], x_sem.at[k])]
        return rows + [
            pltpu.make_async_copy(gate_in.at[d, pl.ds(0, GATE_COLS)], both.at[0, d, pl.ds(0, GATE_COLS)], top_sem.at[k, 0]),
            pltpu.make_async_copy(up_in.at[d, pl.ds(0, GATE_COLS)], both.at[0, d, pl.ds(GATE_COLS, GATE_COLS)], top_sem.at[k, 1]),
        ]

    whole = []
    if blocks > 1:
        whole = [send(x_in[k], x.at[pl.ds(k * size, size)], x_sem, k) for k in range(blocks)]
    for copy in whole:
        copy.start()
    for k in range(PIECES):
        for copy in top(k):
            copy.start()
    for copy in whole:
        copy.wait()
    acc[...] = jnp.zeros_like(acc)

    @pl.loop(0, PIECES)
    def _(k):
        for copy in top(k):
            copy.wait()
        for ahead in (1, 2):

            @pl.when(k == 2 * ahead - 1)
            def _():
                for copy in fetch(ahead):
                    copy.start()

        d = lanes(k, depth)
        acc[...] += dot(x[:, d], both[0, d, :])

    activate(0)

    @pl.loop(1, tiles)
    def _(n):
        for copy in fetch(n):
            copy.wait()

        @pl.when(n + 2 < tiles)
        def _():
            for copy in fetch(n + 2):
                copy.start()

        @pl.when(n + 2 >= tiles)
        def _():
            half = (n + 2 - tiles) * (downs // 2)
            for j in range(downs // 2):
                fetch_down(half + j).start()

        acc[...] = dot(x[...], both[n])
        activate(n)

    @pl.loop(0, downs)
    def _(n):
        fetch_down(n).wait()
        buf[:, lanes(n, DOWN_COLS)] = dot(hidden[...], down[n]).astype(BF16)
        if blocks == 1:
            store(n).start()

    if blocks == 1:

        @pl.loop(0, downs)
        def _(n):
            store(n).wait()

    else:
        stores = []
        for k in range(blocks):
            home = partner(me_ref[1], k, -1)
            stores.append(send(buf.at[pl.ds(k * size, size)], out_ref.at[home], out_sem, k))
            stores[-1].start()
        for copy in stores:
            copy.wait()


def weighted(w_ref, res):
    both = dot(w_ref[...], res)
    half = both.shape[0] // 2
    return both[:half] + both[half:]


def each_piece(res_ref, res, sems):
    cols = parts(res.shape[1], PIECES)
    loads = [send(res_ref.at[:, c], res.at[:, c], sems, j) for j, c in enumerate(cols)]
    for load in loads:
        load.start()
    for j, c in enumerate(cols):
        loads[j].wait()
        yield j, c


def combine_first_kernel(own_w_ref, arr_w_ref, res_ref, own_ref, arr_ref, res, own_buf, arr_buf, in_sems, sems):
    copies = []
    for j, c in each_piece(res_ref, res, in_sems):
        own_buf[:, c] = weighted(own_w_ref, res[:, c])
        arr_buf[:, c] = weighted(arr_w_ref, res[:, c])
        copies.append(send(own_buf.at[:, c], own_ref.at[:, c], sems, 2 * j))
        copies.append(send(arr_buf.at[:, c], arr_ref.at[:, c], sems, 2 * j + 1))
        copies[-2].start()
        copies[-1].start()
    for copy in copies:
        copy.wait()


def with_part(res_ref, part_ref, res, part, in_sems, part_sems):
    cols = parts(res.shape[1], PIECES)
    loads = [send(part_ref.at[:, c], part.at[:, c], part_sems, j) for j, c in enumerate(cols)]
    for load in loads:
        load.start()
    for j, c in each_piece(res_ref, res, in_sems):
        loads[j].wait()
        yield j, c


def combine_own_kernel(w_ref, res_ref, part_ref, out_ref, res, part, in_sems, part_sems):
    for _, c in with_part(res_ref, part_ref, res, part, in_sems, part_sems):
        out_ref[:, c] = part[:, c] + weighted(w_ref, res[:, c])


def combine_arrived_kernel(room, w_ref, res_ref, part_ref, *refs):
    *out_refs, res, part, buf, in_sems, part_sems, sems = refs
    copies = []
    for j, c in with_part(res_ref, part_ref, res, part, in_sems, part_sems):
        buf[:, c] = (part[:, c] + weighted(w_ref, res[:, c])).astype(BF16)
        for k, out_ref in enumerate(out_refs):
            copies.append(send(buf.at[pl.ds(k * room, room), c], out_ref.at[:, c], sems, j * len(out_refs) + k))
            copies[-1].start()
    for copy in copies:
        copy.wait()


def finish_kernel(pick_ref, own_ref, *refs):
    *back_refs, out_ref, buf, sems = refs
    copies = []
    for j, c in enumerate(parts(out_ref.shape[1], PIECES)):
        back = jnp.concatenate([ref[:, c] for ref in back_refs], axis=0)
        buf[:, c] = (own_ref[:, c] + dot_tn(pick_ref[...], back)).astype(BF16)
        copies.append(send(buf.at[:, c], out_ref.at[:, c], sems, j))
        copies[-1].start()
    for copy in copies:
        copy.wait()


GRANT = 24 * 1024 * 1024
FFN_GRANT = 56 * 1024 * 1024


def in_hbm(x):
    return pltpu.with_memory_space_constraint(x, pltpu.HBM)


VM = pl.BlockSpec(memory_space=pltpu.VMEM)
SM = pl.BlockSpec(memory_space=pltpu.SMEM)
HB = pl.BlockSpec(memory_space=pltpu.HBM)
DMA = pltpu.SemaphoreType.DMA


def call(kernel, in_specs, out_specs, out_shape, scratch, flops, size, grant=GRANT):
    return pl.pallas_call(
        kernel,
        in_specs=in_specs,
        out_specs=out_specs,
        out_shape=out_shape,
        scratch_shapes=scratch,
        compiler_params=pltpu.CompilerParams(vmem_limit_bytes=grant),
        cost_estimate=pl.CostEstimate(flops=flops, bytes_accessed=size, transcendentals=0),
    )


def local(tokens, w_gate, w_up, w_down, expert_ids, gate_index, gate_table, spill):
    dp_count = lax.axis_size("dp")
    expert_count = lax.axis_size("expert")
    own_rows, width = tokens.shape[1:]
    column_tokens = spill.shape[1]
    top_count = expert_ids.shape[2]
    experts_all = w_gate.shape[0] * expert_count
    capacity = 3 * own_rows * top_count // (2 * experts_all)
    room = own_rows // 4
    moved = (dp_count - 1) * room
    source_rows = own_rows + moved
    slots = experts_all * capacity
    ff = w_gate.shape[2]
    first = capacity - 8
    cut = experts_all * first
    rest = slots - cut
    me = jnp.stack([lax.axis_index("dp"), lax.axis_index("expert")]).astype(I32)
    own_in = in_hbm(tokens[0])
    spill_rows = spill.reshape(dp_count, own_rows)
    hbm, vmem = pltpu.HBM, pltpu.VMEM
    steps = range(1, dp_count)
    peers = len(steps)

    def shift(blocks, sign):
        sent = {}
        for k in sorted(steps, key=lambda k: abs(dp_count - 2 * k)):
            pairs = [(i, (i + sign * k) % dp_count) for i in range(dp_count)]
            sent[k] = lax.ppermute(blocks[k - 1], "dp", pairs)
        return [sent[k] for k in steps]

    give, own, *outgoing = call(
        functools.partial(spill_kernel, dp_count, room),
        [SM, HB, HB],
        [VM, VM] + [HB] * peers,
        [vmem((moved, own_rows), BF16), vmem((own_rows, width), BF16)] + [hbm((room, width), BF16)] * peers,
        [vmem((dp_count, own_rows), I32), vmem((moved, width), BF16), DMA(()), DMA((PIECES,)), DMA((PIECES * peers,))],
        2 * moved * own_rows * width,
        4 * own_rows * width,
    )(me, in_hbm(spill_rows), own_in)
    arrived = shift(outgoing, 1)

    level_count = gate_table.shape[0]
    index_t = gate_index[0].T
    ids_t = expert_ids[0].T
    matches = index_t[:, None, :] == jnp.arange(level_count, dtype=I32)[None, :, None]
    picked = jnp.sum(jnp.where(matches, gate_table[None, :, None], 0.0), axis=1)
    weight = picked / jnp.sum(picked, axis=0, keepdims=True)
    pick, own_w, arr_w = call(
        functools.partial(route_kernel, dp_count, room, experts_all, capacity, first),
        [SM, VM, VM, VM],
        [VM] * 3,
        [vmem((slots, source_rows), BF16), vmem((2 * own_rows, slots), BF16), vmem((2 * moved, slots), BF16)],
        [],
        2 * column_tokens * column_tokens * 600,
        6 * slots * source_rows,
    )(me, spill_rows, ids_t, weight)

    def exchange(rows):
        shaped = rows.reshape(expert_count, -1, width)
        return lax.all_to_all(shaped, "expert", split_axis=0, concat_axis=0, tiled=True).reshape(-1, width)

    outbound = call(
        build_kernel,
        [VM] * (2 + peers),
        HB,
        hbm((cut, width), BF16),
        [vmem((cut, width), BF16), DMA((PIECES,))],
        2 * cut * source_rows * width,
        2 * (cut + source_rows) * width,
    )(pick[:cut], own, *arrived)
    inbound = exchange(outbound)
    size = rest // expert_count
    blocks = call(
        functools.partial(build_blocks_kernel, size),
        [VM] * (2 + peers),
        [HB] * expert_count,
        [hbm((size, width), BF16)] * expert_count,
        [vmem((rest, width), BF16), DMA((expert_count,))],
        2 * rest * source_rows * width,
        2 * (rest + source_rows) * width,
    )(pick[cut:], own, *arrived)

    def far(k):
        z, y = k // (Y * C), k // C % Y
        return -(min(z, Z - z) + min(y, Y - y))

    landed = {0: blocks[0]}
    for k in sorted(range(1, expert_count), key=far):
        landed[k] = lax.ppermute(blocks[k], "expert", [(i, partner(i, k, 1)) for i in range(expert_count)])

    tiles, downs = ff // GATE_COLS, width // DOWN_COLS

    def experts(inputs, count, out_shape):
        blocks = len(inputs)
        return call(
            functools.partial(ffn_kernel, blocks),
            [SM] + [HB] * (blocks + 3),
            HB,
            hbm(out_shape, BF16),
            [
                vmem((count, width), BF16),
                vmem((tiles, width, 2 * GATE_COLS), BF16),
                vmem((downs, ff, DOWN_COLS), BF16),
                vmem((count, 2 * GATE_COLS), F32),
                vmem((count, ff), BF16),
                vmem((count, width), BF16),
                DMA((max(blocks, PIECES),)),
                DMA((PIECES, 2)),
                DMA((tiles, 2)),
                DMA((downs,)),
                DMA((max(blocks, downs),)),
            ],
            6 * count * width * ff,
            4 * count * width + 6 * width * ff,
            FFN_GRANT,
        )(me, *inputs, w_gate[0], w_up[0], w_down[0])

    outcome = experts([inbound], cut, (cut, width))
    back0 = exchange(outcome)
    arrivals = [in_hbm(landed[k]) for k in range(expert_count)]
    back1 = exchange(experts(arrivals, rest, (expert_count, size, width)))

    part_own, part_arr = call(
        combine_first_kernel,
        [VM, VM, HB],
        [HB] * 2,
        [hbm((own_rows, width), F32), hbm((moved, width), F32)],
        [
            vmem((cut, width), BF16),
            vmem((own_rows, width), F32),
            vmem((moved, width), F32),
            DMA((PIECES,)),
            DMA((2 * PIECES,)),
        ],
        4 * source_rows * cut * width,
        2 * cut * width + 4 * source_rows * width,
    )(own_w[:, :cut], arr_w[:, :cut], in_hbm(back0))
    back1 = in_hbm(back1)
    arrived_parts = call(
        functools.partial(combine_arrived_kernel, room),
        [VM, HB, HB],
        [HB] * peers,
        [hbm((room, width), BF16)] * peers,
        [
            vmem((rest, width), BF16),
            vmem((moved, width), F32),
            vmem((moved, width), BF16),
            DMA((PIECES,)),
            DMA((PIECES,)),
            DMA((PIECES * peers,)),
        ],
        4 * moved * rest * width,
        2 * rest * width + 6 * moved * width,
    )(arr_w[:, cut:], back1, in_hbm(part_arr))
    returned = shift(arrived_parts, -1)
    own_part = call(
        combine_own_kernel,
        [VM, HB, HB],
        VM,
        vmem((own_rows, width), F32),
        [vmem((rest, width), BF16), vmem((own_rows, width), F32), DMA((PIECES,)), DMA((PIECES,))],
        4 * own_rows * rest * width,
        2 * rest * width + 8 * own_rows * width,
    )(own_w[:, cut:], back1, in_hbm(part_own))
    mixed = call(
        finish_kernel,
        [VM] * (2 + peers),
        HB,
        hbm((own_rows, width), BF16),
        [vmem((own_rows, width), BF16), DMA((PIECES,))],
        2 * moved * own_rows * width,
        8 * own_rows * width,
    )(give, own_part, *returned)
    return mixed[None]


def solution(mesh):
    in_specs = (
        P("expert", "dp", None),
        P("expert", None, None),
        P("expert", None, None),
        P("expert", None, None),
        P("expert", None, None),
        P("expert", None, None),
        P(),
        P("expert", None),
    )
    out_specs = P("expert", "dp", None)

    return jax.shard_map(local, mesh=mesh, in_specs=in_specs, out_specs=out_specs, check_vma=False)
```

profile of v0, /device:TPU:0, one launch (start us, length us, event | category | flops | bytes accessed | tf_op | source)
XLA Modules:
  0.0 283.1 jit_solution(18023932323488025556)
XLA Ops:
  0.1 3.2 %shard_map.82 = (bf16[96,128]{1,0:T(8,128)(2,1)S(1)}, bf16[128,4096]{1,0:T(8,128)(2,1)S(1)}, bf16[32,4096]{1,0:T(8,128)(2,1)}, bf16[32,4096]{1,0:T(8,128)(2,1)}, bf16[32,4096]{1,0:T(8,128)(2,1)}) custom-call(s32[2]{0:T(128)S(1)} %pad_add_fusion.me_ref, s32[4,128]{1,0:T(4,128)} %bitcast.19, bf16[128,4096]{1,0:T(8,128)(2,1)} %bitcast.31), custom_call_target="tpu_custom_call" | custom-call | flops 100663296 | bytes 2097152 | tf_op jit(solution)/shard_map/pallas_call | solution.py:415
  5.0 2.7 collective-permute-start.1
  14.1 5.4 %collective-permute-done.1.refs_2_ = bf16[32,4096]{1,0:T(8,128)(2,1)S(1)} collective-permute-done((bf16[32,4096]{1,0:T(8,128)(2,1)}, bf16[32,4096]{1,0:T(8,128)(2,1)S(1)}, u32[]{:S(2)}, u32[]{:S(2)}) %collective-permute-start.1) | collective-permute-done | bytes 262176 | tf_op jit(solution)/shard_map/ppermute | solution.py:412
  19.6 2.5 shard_map.86
  22.1 59.4 %all_to_all.15 = bf16[32,16,4096]{2,1,0:T(8,128)(2,1)} all-to-all(bf16[32,16,4096]{2,1,0:T(8,128)(2,1)} %bitcast.22), channel_id=1, replica_groups=mesh['dp'=4,'expert'=32] {'expert'}, dimensions={0} | all-to-all | bytes 8388608 | tf_op jit(solution)/shard_map/all_to_all | solution.py:444
  81.5 18.7 %shard_map.87 = bf16[512,4096]{1,0:T(8,128)(2,1)} custom-call(s32[2]{0:T(128)} %copy-done.1, bf16[512,4096]{1,0:T(8,128)(2,1)} %bitcast.30, bf16[4096,896]{1,0:T(8,128)(2,1)} %bitcast.23, bf16[4096,896]{1,0:T(8,128)(2,1)} %bitcast.25, bf16[896,4096]{1,0:T(8,128)(2,1)} %bitcast.27), custom_call_target="tpu_custom_call" | custom-call | flops 11274289152 | bytes 30408704 | tf_op jit(solution)/shard_map/pallas_call | solution.py:479
  100.1 4.9 %all-to-all-start.2 = ((bf16[32,16,4096]{2,1,0:T(8,128)(2,1)}), bf16[32,16,4096]{2,1,0:T(8,128)(2,1)}, u32[]{:S(2)}, u32[]{:S(2)}) async-start(bf16[32,16,4096]{2,1,0:T(8,128)(2,1)} %bitcast.29), calls=%async_computation.2 | async-start | bytes 8388608 | tf_op jit(solution)/shard_map/all_to_all | solution.py:444
  115.3 40.9 %collective-permute-done.4.refs_2_ = bf16[8,4096]{1,0:T(8,128)(2,1)S(1)} collective-permute-done((bf16[8,4096]{1,0:T(8,128)(2,1)}, bf16[8,4096]{1,0:T(8,128)(2,1)S(1)}, u32[]{:S(2)}, u32[]{:S(2)}) %collective-permute-start.4) | collective-permute-done | bytes 65568 | tf_op jit(solution)/shard_map/ppermute | solution.py:473
  164.2 4.9 %collective-permute-start.14 = (bf16[8,4096]{1,0:T(8,128)(2,1)}, bf16[8,4096]{1,0:T(8,128)(2,1)S(1)}, u32[]{:S(2)}, u32[]{:S(2)}) collective-permute-start(bf16[8,4096]{1,0:T(8,128)(2,1)} %get-tuple-element.69), channel_id=1, source_target_pairs={{0,12},{1,13},{2,14},{3,15},{4,8},{5,9},{6,10},{7,11},{8,20},{9,21... | collective-permute-start | bytes 196616 | tf_op jit(solution)/shard_map/ppermute | solution.py:473
  169.2 2.6 collective-permute-start.16
  171.7 3.3 %collective-permute-start.17 = (bf16[8,4096]{1,0:T(8,128)(2,1)}, bf16[8,4096]{1,0:T(8,128)(2,1)S(1)}, u32[]{:S(2)}, u32[]{:S(2)}) collective-permute-start(bf16[8,4096]{1,0:T(8,128)(2,1)} %get-tuple-element.72), channel_id=1, source_target_pairs={{0,15},{1,14},{2,9},{3,8},{4,11},{5,10},{6,13},{7,12},{8,23},{9,22... | collective-permute-start | bytes 196616 | tf_op jit(solution)/shard_map/ppermute | solution.py:473
  179.9 6.6 %collective-permute-start.22 = (bf16[8,4096]{1,0:T(8,128)(2,1)}, bf16[8,4096]{1,0:T(8,128)(2,1)S(1)}, u32[]{:S(2)}, u32[]{:S(2)}) collective-permute-start(bf16[8,4096]{1,0:T(8,128)(2,1)} %get-tuple-element.77), channel_id=1, source_target_pairs={{0,20},{1,21},{2,22},{3,23},{4,16},{5,17},{6,18},{7,19},{8,28},{9,... | collective-permute-start | bytes 196616 | tf_op jit(solution)/shard_map/ppermute | solution.py:473
  186.6 3.6 %collective-permute-start.24 = (bf16[8,4096]{1,0:T(8,128)(2,1)}, bf16[8,4096]{1,0:T(8,128)(2,1)S(1)}, u32[]{:S(2)}, u32[]{:S(2)}) collective-permute-start(bf16[8,4096]{1,0:T(8,128)(2,1)} %get-tuple-element.79), channel_id=1, source_target_pairs={{0,22},{1,23},{2,16},{3,17},{4,18},{5,19},{6,20},{7,21},{8,30},{9,... | collective-permute-start | bytes 196616 | tf_op jit(solution)/shard_map/ppermute | solution.py:473
  190.2 3.3 %collective-permute-start.25 = (bf16[8,4096]{1,0:T(8,128)(2,1)}, bf16[8,4096]{1,0:T(8,128)(2,1)S(1)}, u32[]{:S(2)}, u32[]{:S(2)}) collective-permute-start(bf16[8,4096]{1,0:T(8,128)(2,1)} %get-tuple-element.80), channel_id=1, source_target_pairs={{0,23},{1,22},{2,17},{3,16},{4,19},{5,18},{6,21},{7,20},{8,31},{9,... | collective-permute-start | bytes 196616 | tf_op jit(solution)/shard_map/ppermute | solution.py:473
  196.6 5.3 %collective-permute-start.30 = (bf16[8,4096]{1,0:T(8,128)(2,1)}, bf16[8,4096]{1,0:T(8,128)(2,1)S(1)}, u32[]{:S(2)}, u32[]{:S(2)}) collective-permute-start(bf16[8,4096]{1,0:T(8,128)(2,1)} %get-tuple-element.85), channel_id=1, source_target_pairs={{0,28},{1,29},{2,30},{3,31},{4,24},{5,25},{6,26},{7,27},{8,4},{9,5... | collective-permute-start | bytes 196616 | tf_op jit(solution)/shard_map/ppermute | solution.py:473
  202.5 3.3 %collective-permute-start.32 = (bf16[8,4096]{1,0:T(8,128)(2,1)}, bf16[8,4096]{1,0:T(8,128)(2,1)S(1)}, u32[]{:S(2)}, u32[]{:S(2)}) collective-permute-start(bf16[8,4096]{1,0:T(8,128)(2,1)} %get-tuple-element.87), channel_id=1, source_target_pairs={{0,30},{1,31},{2,24},{3,25},{4,26},{5,27},{6,28},{7,29},{8,6},{9,7... | collective-permute-start | bytes 196616 | tf_op jit(solution)/shard_map/ppermute | solution.py:473
  211.5 15.3 %shard_map.85 = bf16[32,8,4096]{2,1,0:T(8,128)(2,1)} custom-call(s32[2]{0:T(128)} %copy-done.1, bf16[8,4096]{1,0:T(8,128)(2,1)} %get-tuple-element.57.refs_0_, bf16[8,4096]{1,0:T(8,128)(2,1)} %copy-done.3, bf16[8,4096]{1,0:T(8,128)(2,1)} %copy-done.4, bf16[8,4096]{1,0:T(8,128)(2,1)} %copy-done.5, bf16[8,4096]{1,0:T(8,128)(2,1)} %copy-done.6, ...), custom_call_target="tpu_custom_call" | custom-call | flops 5637144576 | bytes 26214400 | tf_op jit(solution)/shard_map/pallas_call | solution.py:479
  226.8 5.6 %all-to-all-start = ((bf16[32,8,4096]{2,1,0:T(8,128)(2,1)}), bf16[32,8,4096]{2,1,0:T(8,128)(2,1)}, u32[]{:S(2)}, u32[]{:S(2)}) async-start(bf16[32,8,4096]{2,1,0:T(8,128)(2,1)} %shard_map.85), calls=%async_computation | async-start | bytes 4194304 | tf_op jit(solution)/shard_map/all_to_all | solution.py:444
  232.4 4.7 %shard_map.88 = (f32[128,4096]{1,0:T(8,128)}, f32[96,4096]{1,0:T(8,128)}) custom-call(bf16[256,512]{1,0:T(8,128)(2,1)S(1)} %slice.20.own_w_ref, bf16[192,512]{1,0:T(8,128)(2,1)S(1)} %slice.21.arr_w_ref, bf16[512,4096]{1,0:T(8,128)(2,1)} %bitcast.15.res_ref), custom_call_target="tpu_custom_call" | custom-call | flops 1879048192 | bytes 7864320 | tf_op jit(solution)/shard_map/pallas_call | solution.py:507
  237.1 25.1 %all-to-all-done = bf16[32,8,4096]{2,1,0:T(8,128)(2,1)} async-done(((bf16[32,8,4096]{2,1,0:T(8,128)(2,1)}), bf16[32,8,4096]{2,1,0:T(8,128)(2,1)}, u32[]{:S(2)}, u32[]{:S(2)}) %all-to-all-start) | async-done | bytes 2097184 | tf_op jit(solution)/shard_map/all_to_all | solution.py:444
  262.2 3.1 %shard_map.90 = (bf16[32,4096]{1,0:T(8,128)(2,1)}, bf16[32,4096]{1,0:T(8,128)(2,1)}, bf16[32,4096]{1,0:T(8,128)(2,1)}) custom-call(bf16[192,256]{1,0:T(8,128)(2,1)S(1)} %slice.23.w_ref, bf16[256,4096]{1,0:T(8,128)(2,1)} %bitcast.11.res_ref, f32[96,4096]{1,0:T(8,128)} %get-tuple-element.91.part_ref), custom_call_target="tpu_custom_call" | custom-call | flops 402653184 | bytes 4456448 | tf_op jit(solution)/shard_map/pallas_call | solution.py:523
  269.5 2.5 shard_map.89.own_ref
  272.0 6.1 %collective-permute-done.34.refs_0_ = bf16[32,4096]{1,0:T(8,128)(2,1)S(1)} collective-permute-done((bf16[32,4096]{1,0:T(8,128)(2,1)}, bf16[32,4096]{1,0:T(8,128)(2,1)S(1)}, u32[]{:S(2)}, u32[]{:S(2)}) %collective-permute-start.34) | collective-permute-done | bytes 262176 | tf_op jit(solution)/shard_map/ppermute | solution.py:412
  278.5 3.1 %collective-permute-done.36.refs_2_ = bf16[32,4096]{1,0:T(8,128)(2,1)S(1)} collective-permute-done((bf16[32,4096]{1,0:T(8,128)(2,1)}, bf16[32,4096]{1,0:T(8,128)(2,1)S(1)}, u32[]{:S(2)}, u32[]{:S(2)}) %collective-permute-start.36) | collective-permute-done | bytes 262176 | tf_op jit(solution)/shard_map/ppermute | solution.py:412
  (142 shorter events, 46.4 us)
Async XLA Ops:
  3.3 10.8 %collective-permute-start = (bf16[32,4096]{1,0:T(8,128)(2,1)}, bf16[32,4096]{1,0:T(8,128)(2,1)S(1)}, u32[]{:S(2)}, u32[]{:S(2)}) collective-permute-start(bf16[32,4096]{1,0:T(8,128)(2,1)} %get-tuple-element.54), channel_id=1, source_target_pairs={{0,32},{32,64},{64,96},{96,0},{1,33},{33,65},{65,97},{97,1},{2,34}... | collective-permute-start | bytes 786440 | tf_op jit(solution)/shard_map/ppermute | solution.py:412
  5.0 14.6 %collective-permute-start.1 = (bf16[32,4096]{1,0:T(8,128)(2,1)}, bf16[32,4096]{1,0:T(8,128)(2,1)S(1)}, u32[]{:S(2)}, u32[]{:S(2)}) collective-permute-start(bf16[32,4096]{1,0:T(8,128)(2,1)} %get-tuple-element.55), channel_id=1, source_target_pairs={{0,64},{32,96},{64,0},{96,32},{1,65},{33,97},{65,1},{97,33},{2,66}... | collective-permute-start | bytes 786440 | tf_op jit(solution)/shard_map/ppermute | solution.py:412
  7.7 11.9 %collective-permute-start.2 = (bf16[32,4096]{1,0:T(8,128)(2,1)}, bf16[32,4096]{1,0:T(8,128)(2,1)S(1)}, u32[]{:S(2)}, u32[]{:S(2)}) collective-permute-start(bf16[32,4096]{1,0:T(8,128)(2,1)} %get-tuple-element.56), channel_id=1, source_target_pairs={{0,96},{32,0},{64,32},{96,64},{1,97},{33,1},{65,33},{97,65},{2,98}... | collective-permute-start | bytes 786440 | tf_op jit(solution)/shard_map/ppermute | solution.py:412
  100.1 126.6 %all-to-all-start.2 = ((bf16[32,16,4096]{2,1,0:T(8,128)(2,1)}), bf16[32,16,4096]{2,1,0:T(8,128)(2,1)}, u32[]{:S(2)}, u32[]{:S(2)}) async-start(bf16[32,16,4096]{2,1,0:T(8,128)(2,1)} %bitcast.29), calls=%async_computation.2 | async-start | bytes 8388608 | tf_op jit(solution)/shard_map/all_to_all | solution.py:444
  107.5 48.8 %collective-permute-start.4 = (bf16[8,4096]{1,0:T(8,128)(2,1)}, bf16[8,4096]{1,0:T(8,128)(2,1)S(1)}, u32[]{:S(2)}, u32[]{:S(2)}) collective-permute-start(bf16[8,4096]{1,0:T(8,128)(2,1)} %get-tuple-element.59), channel_id=1, source_target_pairs={{0,2},{1,3},{2,4},{3,5},{4,6},{5,7},{6,0},{7,1},{8,10},{9,11},{10,... | collective-permute-start | bytes 196616 | tf_op jit(solution)/shard_map/ppermute | solution.py:473
  109.1 48.6 %collective-permute-start.5 = (bf16[8,4096]{1,0:T(8,128)(2,1)}, bf16[8,4096]{1,0:T(8,128)(2,1)S(1)}, u32[]{:S(2)}, u32[]{:S(2)}) collective-permute-start(bf16[8,4096]{1,0:T(8,128)(2,1)} %get-tuple-element.60), channel_id=1, source_target_pairs={{0,3},{1,2},{2,5},{3,4},{4,7},{5,6},{6,1},{7,0},{8,11},{9,10},{10,... | collective-permute-start | bytes 196616 | tf_op jit(solution)/shard_map/ppermute | solution.py:473
  110.3 51.1 %collective-permute-start.6 = (bf16[8,4096]{1,0:T(8,128)(2,1)}, bf16[8,4096]{1,0:T(8,128)(2,1)S(1)}, u32[]{:S(2)}, u32[]{:S(2)}) collective-permute-start(bf16[8,4096]{1,0:T(8,128)(2,1)} %get-tuple-element.61), channel_id=1, source_target_pairs={{0,4},{1,5},{2,6},{3,7},{4,0},{5,1},{6,2},{7,3},{8,12},{9,13},{10,... | collective-permute-start | bytes 196616 | tf_op jit(solution)/shard_map/ppermute | solution.py:473
  111.9 49.9 %collective-permute-start.7 = (bf16[8,4096]{1,0:T(8,128)(2,1)}, bf16[8,4096]{1,0:T(8,128)(2,1)S(1)}, u32[]{:S(2)}, u32[]{:S(2)}) collective-permute-start(bf16[8,4096]{1,0:T(8,128)(2,1)} %get-tuple-element.62), channel_id=1, source_target_pairs={{0,5},{1,4},{2,7},{3,6},{4,1},{5,0},{6,3},{7,2},{8,13},{9,12},{10,... | collective-permute-start | bytes 196616 | tf_op jit(solution)/shard_map/ppermute | solution.py:473
  113.6 48.4 %collective-permute-start.8 = (bf16[8,4096]{1,0:T(8,128)(2,1)}, bf16[8,4096]{1,0:T(8,128)(2,1)S(1)}, u32[]{:S(2)}, u32[]{:S(2)}) collective-permute-start(bf16[8,4096]{1,0:T(8,128)(2,1)} %get-tuple-element.63), channel_id=1, source_target_pairs={{0,6},{1,7},{2,0},{3,1},{4,2},{5,3},{6,4},{7,5},{8,14},{9,15},{10,... | collective-permute-start | bytes 196616 | tf_op jit(solution)/shard_map/ppermute | solution.py:473
  157.7 11.3 %collective-permute-start.10 = (bf16[8,4096]{1,0:T(8,128)(2,1)}, bf16[8,4096]{1,0:T(8,128)(2,1)S(1)}, u32[]{:S(2)}, u32[]{:S(2)}) collective-permute-start(bf16[8,4096]{1,0:T(8,128)(2,1)} %get-tuple-element.65), channel_id=1, source_target_pairs={{0,8},{1,9},{2,10},{3,11},{4,12},{5,13},{6,14},{7,15},{8,16},{9,17... | collective-permute-start | bytes 196616 | tf_op jit(solution)/shard_map/ppermute | solution.py:473
  162.0 13.1 %collective-permute-start.13 = (bf16[8,4096]{1,0:T(8,128)(2,1)}, bf16[8,4096]{1,0:T(8,128)(2,1)S(1)}, u32[]{:S(2)}, u32[]{:S(2)}) collective-permute-start(bf16[8,4096]{1,0:T(8,128)(2,1)} %get-tuple-element.68), channel_id=1, source_target_pairs={{0,11},{1,10},{2,13},{3,12},{4,15},{5,14},{6,9},{7,8},{8,19},{9,18... | collective-permute-start | bytes 196616 | tf_op jit(solution)/shard_map/ppermute | solution.py:473
  164.2 12.8 %collective-permute-start.14 = (bf16[8,4096]{1,0:T(8,128)(2,1)}, bf16[8,4096]{1,0:T(8,128)(2,1)S(1)}, u32[]{:S(2)}, u32[]{:S(2)}) collective-permute-start(bf16[8,4096]{1,0:T(8,128)(2,1)} %get-tuple-element.69), channel_id=1, source_target_pairs={{0,12},{1,13},{2,14},{3,15},{4,8},{5,9},{6,10},{7,11},{8,20},{9,21... | collective-permute-start | bytes 196616 | tf_op jit(solution)/shard_map/ppermute | solution.py:473
  169.2 10.0 %collective-permute-start.16 = (bf16[8,4096]{1,0:T(8,128)(2,1)}, bf16[8,4096]{1,0:T(8,128)(2,1)S(1)}, u32[]{:S(2)}, u32[]{:S(2)}) collective-permute-start(bf16[8,4096]{1,0:T(8,128)(2,1)} %get-tuple-element.71), channel_id=1, source_target_pairs={{0,14},{1,15},{2,8},{3,9},{4,10},{5,11},{6,12},{7,13},{8,22},{9,23... | collective-permute-start | bytes 196616 | tf_op jit(solution)/shard_map/ppermute | solution.py:473
  175.0 11.5 %collective-permute-start.18 = (bf16[8,4096]{1,0:T(8,128)(2,1)}, bf16[8,4096]{1,0:T(8,128)(2,1)S(1)}, u32[]{:S(2)}, u32[]{:S(2)}) collective-permute-start(bf16[8,4096]{1,0:T(8,128)(2,1)} %get-tuple-element.73), channel_id=1, source_target_pairs={{0,16},{1,17},{2,18},{3,19},{4,20},{5,21},{6,22},{7,23},{8,24},{9,... | collective-permute-start | bytes 196616 | tf_op jit(solution)/shard_map/ppermute | solution.py:473
  177.2 13.0 %collective-permute-start.20 = (bf16[8,4096]{1,0:T(8,128)(2,1)}, bf16[8,4096]{1,0:T(8,128)(2,1)S(1)}, u32[]{:S(2)}, u32[]{:S(2)}) collective-permute-start(bf16[8,4096]{1,0:T(8,128)(2,1)} %get-tuple-element.75), channel_id=1, source_target_pairs={{0,18},{1,19},{2,20},{3,21},{4,22},{5,23},{6,16},{7,17},{8,26},{9,... | collective-permute-start | bytes 196616 | tf_op jit(solution)/shard_map/ppermute | solution.py:473
  179.2 14.3 %collective-permute-start.21 = (bf16[8,4096]{1,0:T(8,128)(2,1)}, bf16[8,4096]{1,0:T(8,128)(2,1)S(1)}, u32[]{:S(2)}, u32[]{:S(2)}) collective-permute-start(bf16[8,4096]{1,0:T(8,128)(2,1)} %get-tuple-element.76), channel_id=1, source_target_pairs={{0,19},{1,18},{2,21},{3,20},{4,23},{5,22},{6,17},{7,16},{8,27},{9,... | collective-permute-start | bytes 196616 | tf_op jit(solution)/shard_map/ppermute | solution.py:473
  179.9 14.9 %collective-permute-start.22 = (bf16[8,4096]{1,0:T(8,128)(2,1)}, bf16[8,4096]{1,0:T(8,128)(2,1)S(1)}, u32[]{:S(2)}, u32[]{:S(2)}) collective-permute-start(bf16[8,4096]{1,0:T(8,128)(2,1)} %get-tuple-element.77), channel_id=1, source_target_pairs={{0,20},{1,21},{2,22},{3,23},{4,16},{5,17},{6,18},{7,19},{8,28},{9,... | collective-permute-start | bytes 196616 | tf_op jit(solution)/shard_map/ppermute | solution.py:473
  194.9 10.9 %collective-permute-start.28 = (bf16[8,4096]{1,0:T(8,128)(2,1)}, bf16[8,4096]{1,0:T(8,128)(2,1)S(1)}, u32[]{:S(2)}, u32[]{:S(2)}) collective-permute-start(bf16[8,4096]{1,0:T(8,128)(2,1)} %get-tuple-element.83), channel_id=1, source_target_pairs={{0,26},{1,27},{2,28},{3,29},{4,30},{5,31},{6,24},{7,25},{8,2},{9,3... | collective-permute-start | bytes 196616 | tf_op jit(solution)/shard_map/ppermute | solution.py:473
  196.0 11.2 %collective-permute-start.29 = (bf16[8,4096]{1,0:T(8,128)(2,1)}, bf16[8,4096]{1,0:T(8,128)(2,1)S(1)}, u32[]{:S(2)}, u32[]{:S(2)}) collective-permute-start(bf16[8,4096]{1,0:T(8,128)(2,1)} %get-tuple-element.84), channel_id=1, source_target_pairs={{0,27},{1,26},{2,29},{3,28},{4,31},{5,30},{6,25},{7,24},{8,3},{9,2... | collective-permute-start | bytes 196616 | tf_op jit(solution)/shard_map/ppermute | solution.py:473
  196.6 10.5 %collective-permute-start.30 = (bf16[8,4096]{1,0:T(8,128)(2,1)}, bf16[8,4096]{1,0:T(8,128)(2,1)S(1)}, u32[]{:S(2)}, u32[]{:S(2)}) collective-permute-start(bf16[8,4096]{1,0:T(8,128)(2,1)} %get-tuple-element.85), channel_id=1, source_target_pairs={{0,28},{1,29},{2,30},{3,31},{4,24},{5,25},{6,26},{7,27},{8,4},{9,5... | collective-permute-start | bytes 196616 | tf_op jit(solution)/shard_map/ppermute | solution.py:473
  226.8 35.4 %all-to-all-start = ((bf16[32,8,4096]{2,1,0:T(8,128)(2,1)}), bf16[32,8,4096]{2,1,0:T(8,128)(2,1)}, u32[]{:S(2)}, u32[]{:S(2)}) async-start(bf16[32,8,4096]{2,1,0:T(8,128)(2,1)} %shard_map.85), calls=%async_computation | async-start | bytes 4194304 | tf_op jit(solution)/shard_map/all_to_all | solution.py:444
  265.3 12.8 %collective-permute-start.34 = (bf16[32,4096]{1,0:T(8,128)(2,1)}, bf16[32,4096]{1,0:T(8,128)(2,1)S(1)}, u32[]{:S(2)}, u32[]{:S(2)}) collective-permute-start(bf16[32,4096]{1,0:T(8,128)(2,1)} %get-tuple-element.92), channel_id=1, source_target_pairs={{0,96},{32,0},{64,32},{96,64},{1,97},{33,1},{65,33},{97,65},{2,98}... | collective-permute-start | bytes 786440 | tf_op jit(solution)/shard_map/ppermute | solution.py:412
  267.6 10.9 %collective-permute-start.35 = (bf16[32,4096]{1,0:T(8,128)(2,1)}, bf16[32,4096]{1,0:T(8,128)(2,1)S(1)}, u32[]{:S(2)}, u32[]{:S(2)}) collective-permute-start(bf16[32,4096]{1,0:T(8,128)(2,1)} %get-tuple-element.93), channel_id=1, source_target_pairs={{0,64},{32,96},{64,0},{96,32},{1,65},{33,97},{65,1},{97,33},{2,66}... | collective-permute-start | bytes 786440 | tf_op jit(solution)/shard_map/ppermute | solution.py:412
  268.8 12.9 %collective-permute-start.36 = (bf16[32,4096]{1,0:T(8,128)(2,1)}, bf16[32,4096]{1,0:T(8,128)(2,1)S(1)}, u32[]{:S(2)}, u32[]{:S(2)}) collective-permute-start(bf16[32,4096]{1,0:T(8,128)(2,1)} %get-tuple-element.94), channel_id=1, source_target_pairs={{0,32},{32,64},{64,96},{96,0},{1,33},{33,65},{65,97},{97,1},{2,34}... | collective-permute-start | bytes 786440 | tf_op jit(solution)/shard_map/ppermute | solution.py:412
  (49 other events, 1013.7 us)
where the time goes:
time: 284 us; the launch traced here: 283 us
  waiting for transfers between devices  86.6 us (30%)
  starting transfers between devices  77.4 us (27%)
  blocking collectives  59.4 us (21%)
  Pallas kernels  56 us (20%)
    all_to_all x1, blocking collectives, exchange(): lax.all_to_all(shaped, 'expert', split_axis=0, concat_axis=0, tiled=True)  59.4 us
    ppermute x31, starting transfers between devices, local(): lax.ppermute(blocks[k], 'expert', [(i, partner(i, k, 1)) for i in range(e...  57 us
    ppermute x31, waiting for transfers between devices, local(): lax.ppermute(blocks[k], 'expert', [(i, partner(i, k, 1)) for i in range(e...  46.5 us
    pallas_call x2, Pallas kernels, experts(): call(functools.partial(ffn_kernel, blocks), [SM] + [HB] * (blocks + 3), H...  33.9 us
    all_to_all x2, waiting for transfers between devices, exchange(): lax.all_to_all(shaped, 'expert', split_axis=0, concat_axis=0, tiled=True)  25.1 us
    ppermute x6, waiting for transfers between devices, shift(): sent[k] = lax.ppermute(blocks[k - 1], 'dp', pairs)  15.1 us
    all_to_all x2, starting transfers between devices, exchange(): lax.all_to_all(shaped, 'expert', split_axis=0, concat_axis=0, tiled=True)  10.4 us
    ppermute x6, starting transfers between devices, shift(): sent[k] = lax.ppermute(blocks[k - 1], 'dp', pairs)  9.98 us
  transfers between devices with their start and end apart: 39, of which 9 were waited for; matrix products, arithmetic and copies ran while one was open for 0% of the time, Pallas kernels for 10%

commit v1 on v0

--- a/solution.py
+++ b/solution.py
@@ -178,13 +178,25 @@
         copy.wait()
 
 
+def regroup_kernel(size, *refs):
+    *in_refs, out_ref, buf, in_sems, out_sem = refs
+    loads = [send(ref.at[pl.ds(size, size)], buf.at[pl.ds(j * size, size)], in_sems, j) for j, ref in enumerate(in_refs)]
+    for load in loads:
+        load.start()
+    for load in loads:
+        load.wait()
+    store = send(buf, out_ref, out_sem, 0)
+    store.start()
+    store.wait()
+
+
 GATE_COLS = 128
 DOWN_COLS = 1024
 
 
-def ffn_kernel(blocks, me_ref, *refs):
-    x_in, (gate_in, up_in, down_in, out_ref, x, both, down, acc, hidden, buf) = refs[:blocks], refs[blocks : blocks + 10]
-    x_sem, top_sem, both_sem, down_sem, out_sem = refs[blocks + 10 :]
+def ffn_kernel(blocks, inputs, me_ref, *refs):
+    x_in, (gate_in, up_in, down_in, out_ref, x, both, down, acc, hidden, buf) = refs[:inputs], refs[inputs : inputs + 10]
+    x_sem, top_sem, both_sem, down_sem, out_sem = refs[inputs + 10 :]
     depth = x.shape[1] // PIECES
     tiles, downs = both.shape[0], down.shape[0]
     size = x.shape[0] // blocks
@@ -220,7 +232,10 @@
 
     whole = []
     if blocks > 1:
-        whole = [send(x_in[k], x.at[pl.ds(k * size, size)], x_sem, k) for k in range(blocks)]
+        for k in range(blocks):
+            chip, core = k // C, k % C
+            ref, row = (x_in[-1], chip * size) if core else (x_in[chip], 0)
+            whole.append(send(ref.at[pl.ds(row, size)], x.at[pl.ds(k * size, size)], x_sem, k))
     for copy in whole:
         copy.start()
     for k in range(PIECES):
@@ -454,12 +469,13 @@
     )(pick[:cut], own, *arrived)
     inbound = exchange(outbound)
     size = rest // expert_count
+    chips = expert_count // C
     blocks = call(
-        functools.partial(build_blocks_kernel, size),
+        functools.partial(build_blocks_kernel, C * size),
         [VM] * (2 + peers),
-        [HB] * expert_count,
-        [hbm((size, width), BF16)] * expert_count,
-        [vmem((rest, width), BF16), DMA((expert_count,))],
+        [HB] * chips,
+        [hbm((C * size, width), BF16)] * chips,
+        [vmem((rest, width), BF16), DMA((chips,))],
         2 * rest * source_rows * width,
         2 * (rest + source_rows) * width,
     )(pick[cut:], own, *arrived)
@@ -468,17 +484,29 @@
         z, y = k // (Y * C), k // C % Y
         return -(min(z, Z - z) + min(y, Y - y))
 
-    landed = {0: blocks[0]}
-    for k in sorted(range(1, expert_count), key=far):
-        landed[k] = lax.ppermute(blocks[k], "expert", [(i, partner(i, k, 1)) for i in range(expert_count)])
+    landed = {0: in_hbm(blocks[0])}
+    for j in sorted(range(1, chips), key=lambda j: far(j * C)):
+        pairs = [(i, partner(i, j * C, 1)) for i in range(expert_count)]
+        landed[j] = in_hbm(lax.ppermute(blocks[j], "expert", pairs))
+    landed = [landed[j] for j in range(chips)]
+    other = call(
+        functools.partial(regroup_kernel, size),
+        [HB] * chips,
+        HB,
+        hbm((chips * size, width), BF16),
+        [vmem((chips * size, width), BF16), DMA((chips,)), DMA((1,))],
+        1000 * rest * width,
+        2 * rest * width,
+    )(*landed)
+    swapped = lax.ppermute(other, "expert", [(i, partner(i, 1, 1)) for i in range(expert_count)])
+    arrivals = [*landed, in_hbm(swapped)]
 
     tiles, downs = ff // GATE_COLS, width // DOWN_COLS
 
-    def experts(inputs, count, out_shape):
-        blocks = len(inputs)
+    def experts(inputs, blocks, count, out_shape):
         return call(
-            functools.partial(ffn_kernel, blocks),
-            [SM] + [HB] * (blocks + 3),
+            functools.partial(ffn_kernel, blocks, len(inputs)),
+            [SM] + [HB] * (len(inputs) + 3),
             HB,
             hbm(out_shape, BF16),
             [
@@ -499,10 +527,9 @@
             FFN_GRANT,
         )(me, *inputs, w_gate[0], w_up[0], w_down[0])
 
-    outcome = experts([inbound], cut, (cut, width))
+    outcome = experts([inbound], 1, cut, (cut, width))
     back0 = exchange(outcome)
-    arrivals = [in_hbm(landed[k]) for k in range(expert_count)]
-    back1 = exchange(experts(arrivals, rest, (expert_count, size, width)))
+    back1 = exchange(experts(arrivals, expert_count, rest, (expert_count, size, width)))
 
     part_own, part_arr = call(
         combine_first_kernel,

time: 284 us -> 276 us (0.972)
  starting transfers between devices: 77.4 us -> 47 us
  waiting for transfers between devices: 86.6 us -> 105 us
    ppermute x31 -> x16, starting transfers between devices: 57 us -> 27.2 us  [the longest x15 27.1 us: local(): landed[j] = in_hbm(lax.ppermute(blocks[j], 'expert', pairs))]
    ppermute x31 -> x16, waiting for transfers between devices: 46.5 us -> 64.6 us  [the longest x15 61.7 us: local(): landed[j] = in_hbm(lax.ppermute(blocks[j], 'expert', pairs))]
    pallas_call x3 -> x4, Pallas kernels: 36.2 us -> 38.4 us  [the longest x2 33.9 us: experts(): call(functools.partial(ffn_kernel, blocks, len(inputs)), [SM] + [HB] * (l...]
  transfers between devices with their start and end apart: 39 -> 24, of which waited for: 9 -> 13; matrix products, arithmetic and copies ran while one was open for 0% -> 0% of each run, Pallas kernels for 10% -> 11%
where the time goes in v1:
time: 276 us; the launch traced here: 274 us
  waiting for transfers between devices  105 us (38%)
  blocking collectives  59.4 us (22%)
  Pallas kernels  58.2 us (21%)
  starting transfers between devices  47 us (17%)
  local copies, waits for them, and re-layouts  3.02 us (1%)
    ppermute x15, waiting for transfers between devices, local(): landed[j] = in_hbm(lax.ppermute(blocks[j], 'expert', pairs))  61.7 us
    all_to_all x1, blocking collectives, exchange(): lax.all_to_all(shaped, 'expert', split_axis=0, concat_axis=0, tiled=True)  59.4 us
    pallas_call x2, Pallas kernels, experts(): call(functools.partial(ffn_kernel, blocks, len(inputs)), [SM] + [HB] * (l...  33.9 us
    ppermute x15, starting transfers between devices, local(): landed[j] = in_hbm(lax.ppermute(blocks[j], 'expert', pairs))  27.1 us
    all_to_all x2, waiting for transfers between devices, exchange(): lax.all_to_all(shaped, 'expert', split_axis=0, concat_axis=0, tiled=True)  25.3 us
    ppermute x6, waiting for transfers between devices, shift(): sent[k] = lax.ppermute(blocks[k - 1], 'dp', pairs)  15.2 us
    ppermute x6, starting transfers between devices, shift(): sent[k] = lax.ppermute(blocks[k - 1], 'dp', pairs)  9.97 us
    all_to_all x2, starting transfers between devices, exchange(): lax.all_to_all(shaped, 'expert', split_axis=0, concat_axis=0, tiled=True)  9.85 us
  transfers between devices with their start and end apart: 24, of which 13 were waited for; matrix products, arithmetic and copies ran while one was open for 0% of the time, Pallas kernels for 11%

profile of v1, /device:TPU:0, one launch (start us, length us, event | category | flops | bytes accessed | tf_op | source)
XLA Modules:
  0.0 274.4 jit_solution(9030341039838782838)
XLA Ops:
  0.1 3.2 %shard_map.82 = (bf16[96,128]{1,0:T(8,128)(2,1)S(1)}, bf16[128,4096]{1,0:T(8,128)(2,1)S(1)}, bf16[32,4096]{1,0:T(8,128)(2,1)}, bf16[32,4096]{1,0:T(8,128)(2,1)}, bf16[32,4096]{1,0:T(8,128)(2,1)}) custom-call(s32[2]{0:T(128)S(1)} %pad_add_fusion.me_ref, s32[4,128]{1,0:T(4,128)} %bitcast.19, bf16[128,4096]{1,0:T(8,128)(2,1)} %bitcast.31), custom_call_target="tpu_custom_call" | custom-call | flops 100663296 | bytes 2097152 | tf_op jit(solution)/shard_map/pallas_call | solution.py:430
  5.0 2.7 collective-permute-start.1
  14.1 5.4 %collective-permute-done.1.refs_2_ = bf16[32,4096]{1,0:T(8,128)(2,1)S(1)} collective-permute-done((bf16[32,4096]{1,0:T(8,128)(2,1)}, bf16[32,4096]{1,0:T(8,128)(2,1)S(1)}, u32[]{:S(2)}, u32[]{:S(2)}) %collective-permute-start.1) | collective-permute-done | bytes 262176 | tf_op jit(solution)/shard_map/ppermute | solution.py:427
  22.1 59.4 %all_to_all.15 = bf16[32,16,4096]{2,1,0:T(8,128)(2,1)} all-to-all(bf16[32,16,4096]{2,1,0:T(8,128)(2,1)} %bitcast.22), channel_id=1, replica_groups=mesh['dp'=4,'expert'=32] {'expert'}, dimensions={0} | all-to-all | bytes 8388608 | tf_op jit(solution)/shard_map/all_to_all | solution.py:459
  81.5 18.6 %shard_map.88 = bf16[512,4096]{1,0:T(8,128)(2,1)} custom-call(s32[2]{0:T(128)} %copy-done, bf16[512,4096]{1,0:T(8,128)(2,1)} %bitcast.30, bf16[4096,896]{1,0:T(8,128)(2,1)} %bitcast.23, bf16[4096,896]{1,0:T(8,128)(2,1)} %bitcast.25, bf16[896,4096]{1,0:T(8,128)(2,1)} %bitcast.27), custom_call_target="tpu_custom_call" | custom-call | flops 11274289152 | bytes 30408704 | tf_op jit(solution)/shard_map/pallas_call | solution.py:507
  100.1 4.9 %all-to-all-start.2 = ((bf16[32,16,4096]{2,1,0:T(8,128)(2,1)}), bf16[32,16,4096]{2,1,0:T(8,128)(2,1)}, u32[]{:S(2)}, u32[]{:S(2)}) async-start(bf16[32,16,4096]{2,1,0:T(8,128)(2,1)} %bitcast.29), calls=%async_computation.2 | async-start | bytes 8388608 | tf_op jit(solution)/shard_map/all_to_all | solution.py:459
  108.8 2.7 collective-permute-start.4
  116.0 41.6 %collective-permute-done.3.refs_1_ = bf16[16,4096]{1,0:T(8,128)(2,1)S(1)} collective-permute-done((bf16[16,4096]{1,0:T(8,128)(2,1)}, bf16[16,4096]{1,0:T(8,128)(2,1)S(1)}, u32[]{:S(2)}, u32[]{:S(2)}) %collective-permute-start.3) | collective-permute-done | bytes 131104 | tf_op jit(solution)/shard_map/ppermute | solution.py:490
  157.6 3.3 %collective-permute-start.8 = (bf16[16,4096]{1,0:T(8,128)(2,1)}, bf16[16,4096]{1,0:T(8,128)(2,1)S(1)}, u32[]{:S(2)}, u32[]{:S(2)}) collective-permute-start(bf16[16,4096]{1,0:T(8,128)(2,1)} %get-tuple-element.47), channel_id=1, source_target_pairs={{0,12},{1,13},{2,14},{3,15},{4,8},{5,9},{6,10},{7,11},{8,20},{9,21... | collective-permute-start | bytes 393224 | tf_op jit(solution)/shard_map/ppermute | solution.py:490
  163.2 2.6 collective-permute-start.10
  165.8 3.3 %collective-permute-start.11 = (bf16[16,4096]{1,0:T(8,128)(2,1)}, bf16[16,4096]{1,0:T(8,128)(2,1)S(1)}, u32[]{:S(2)}, u32[]{:S(2)}) collective-permute-start(bf16[16,4096]{1,0:T(8,128)(2,1)} %get-tuple-element.50), channel_id=1, source_target_pairs={{0,18},{1,19},{2,20},{3,21},{4,22},{5,23},{6,16},{7,17},{8,26},{9,... | collective-permute-start | bytes 393224 | tf_op jit(solution)/shard_map/ppermute | solution.py:490
  175.5 7.6 %collective-permute-done.10.refs_8_ = bf16[16,4096]{1,0:T(8,128)(2,1)S(1)} collective-permute-done((bf16[16,4096]{1,0:T(8,128)(2,1)}, bf16[16,4096]{1,0:T(8,128)(2,1)S(1)}, u32[]{:S(2)}, u32[]{:S(2)}) %collective-permute-start.10) | collective-permute-done | bytes 131104 | tf_op jit(solution)/shard_map/ppermute | solution.py:490
  183.2 3.6 %collective-permute-start.16 = (bf16[16,4096]{1,0:T(8,128)(2,1)}, bf16[16,4096]{1,0:T(8,128)(2,1)S(1)}, u32[]{:S(2)}, u32[]{:S(2)}) collective-permute-start(bf16[16,4096]{1,0:T(8,128)(2,1)} %get-tuple-element.55), channel_id=1, source_target_pairs={{0,28},{1,29},{2,30},{3,31},{4,24},{5,25},{6,26},{7,27},{8,4},{9,5... | collective-permute-start | bytes 393224 | tf_op jit(solution)/shard_map/ppermute | solution.py:490
  187.8 3.6 %collective-permute-done.15.refs_13_ = bf16[16,4096]{1,0:T(8,128)(2,1)S(1)} collective-permute-done((bf16[16,4096]{1,0:T(8,128)(2,1)}, bf16[16,4096]{1,0:T(8,128)(2,1)S(1)}, u32[]{:S(2)}, u32[]{:S(2)}) %collective-permute-start.15) | collective-permute-done | bytes 131104 | tf_op jit(solution)/shard_map/ppermute | solution.py:490
  191.4 4.2 %collective-permute-done.16.refs_14_ = bf16[16,4096]{1,0:T(8,128)(2,1)S(1)} collective-permute-done((bf16[16,4096]{1,0:T(8,128)(2,1)}, bf16[16,4096]{1,0:T(8,128)(2,1)S(1)}, u32[]{:S(2)}, u32[]{:S(2)}) %collective-permute-start.16) | collective-permute-done | bytes 131104 | tf_op jit(solution)/shard_map/ppermute | solution.py:490
  199.2 2.9 %collective-permute-done.18.refs_16_ = bf16[128,4096]{1,0:T(8,128)(2,1)S(1)} collective-permute-done((bf16[128,4096]{1,0:T(8,128)(2,1)}, bf16[128,4096]{1,0:T(8,128)(2,1)S(1)}, u32[]{:S(2)}, u32[]{:S(2)}) %collective-permute-start.18) | collective-permute-done | bytes 1048608 | tf_op jit(solution)/shard_map/ppermute | solution.py:501
  203.0 15.3 %shard_map.86 = bf16[32,8,4096]{2,1,0:T(8,128)(2,1)} custom-call(s32[2]{0:T(128)} %copy-done, bf16[16,4096]{1,0:T(8,128)(2,1)} %get-tuple-element.41.refs_0_, bf16[16,4096]{1,0:T(8,128)(2,1)} %copy-done.4, bf16[16,4096]{1,0:T(8,128)(2,1)} %copy-done.5, bf16[16,4096]{1,0:T(8,128)(2,1)} %copy-done.6, bf16[16,4096]{1,0:T(8,128)(2,1)} %copy-done.7, ...), custom_call_target="tpu_custom_call" | custom-call | flops 5637144576 | bytes 26214400 | tf_op jit(solution)/shard_map/pallas_call | solution.py:507
  218.3 5.0 %all-to-all-start = ((bf16[32,8,4096]{2,1,0:T(8,128)(2,1)}), bf16[32,8,4096]{2,1,0:T(8,128)(2,1)}, u32[]{:S(2)}, u32[]{:S(2)}) async-start(bf16[32,8,4096]{2,1,0:T(8,128)(2,1)} %shard_map.86), calls=%async_computation | async-start | bytes 4194304 | tf_op jit(solution)/shard_map/all_to_all | solution.py:459
  223.4 4.7 %shard_map.89 = (f32[128,4096]{1,0:T(8,128)}, f32[96,4096]{1,0:T(8,128)}) custom-call(bf16[256,512]{1,0:T(8,128)(2,1)S(1)} %slice.20.own_w_ref, bf16[192,512]{1,0:T(8,128)(2,1)S(1)} %slice.21.arr_w_ref, bf16[512,4096]{1,0:T(8,128)(2,1)} %bitcast.15.res_ref), custom_call_target="tpu_custom_call" | custom-call | flops 1879048192 | bytes 7864320 | tf_op jit(solution)/shard_map/pallas_call | solution.py:534
  228.0 25.3 %all-to-all-done = bf16[32,8,4096]{2,1,0:T(8,128)(2,1)} async-done(((bf16[32,8,4096]{2,1,0:T(8,128)(2,1)}), bf16[32,8,4096]{2,1,0:T(8,128)(2,1)}, u32[]{:S(2)}, u32[]{:S(2)}) %all-to-all-start) | async-done | bytes 2097184 | tf_op jit(solution)/shard_map/all_to_all | solution.py:459
  253.3 3.1 %shard_map.91 = (bf16[32,4096]{1,0:T(8,128)(2,1)}, bf16[32,4096]{1,0:T(8,128)(2,1)}, bf16[32,4096]{1,0:T(8,128)(2,1)}) custom-call(bf16[192,256]{1,0:T(8,128)(2,1)S(1)} %slice.23.w_ref, bf16[256,4096]{1,0:T(8,128)(2,1)} %bitcast.11.res_ref, f32[96,4096]{1,0:T(8,128)} %get-tuple-element.59.part_ref), custom_call_target="tpu_custom_call" | custom-call | flops 402653184 | bytes 4456448 | tf_op jit(solution)/shard_map/pallas_call | solution.py:550
  260.6 2.5 shard_map.90.own_ref
  263.2 6.2 %collective-permute-done.19.refs_0_ = bf16[32,4096]{1,0:T(8,128)(2,1)S(1)} collective-permute-done((bf16[32,4096]{1,0:T(8,128)(2,1)}, bf16[32,4096]{1,0:T(8,128)(2,1)S(1)}, u32[]{:S(2)}, u32[]{:S(2)}) %collective-permute-start.19) | collective-permute-done | bytes 262176 | tf_op jit(solution)/shard_map/ppermute | solution.py:427
  269.7 3.2 %collective-permute-done.21.refs_2_ = bf16[32,4096]{1,0:T(8,128)(2,1)S(1)} collective-permute-done((bf16[32,4096]{1,0:T(8,128)(2,1)}, bf16[32,4096]{1,0:T(8,128)(2,1)S(1)}, u32[]{:S(2)}, u32[]{:S(2)}) %collective-permute-start.21) | collective-permute-done | bytes 262176 | tf_op jit(solution)/shard_map/ppermute | solution.py:427
  (83 shorter events, 38.8 us)
Async XLA Ops:
  3.3 10.8 %collective-permute-start = (bf16[32,4096]{1,0:T(8,128)(2,1)}, bf16[32,4096]{1,0:T(8,128)(2,1)S(1)}, u32[]{:S(2)}, u32[]{:S(2)}) collective-permute-start(bf16[32,4096]{1,0:T(8,128)(2,1)} %get-tuple-element.38), channel_id=1, source_target_pairs={{0,32},{32,64},{64,96},{96,0},{1,33},{33,65},{65,97},{97,1},{2,34}... | collective-permute-start | bytes 786440 | tf_op jit(solution)/shard_map/ppermute | solution.py:427
  5.0 14.6 %collective-permute-start.1 = (bf16[32,4096]{1,0:T(8,128)(2,1)}, bf16[32,4096]{1,0:T(8,128)(2,1)S(1)}, u32[]{:S(2)}, u32[]{:S(2)}) collective-permute-start(bf16[32,4096]{1,0:T(8,128)(2,1)} %get-tuple-element.39), channel_id=1, source_target_pairs={{0,64},{32,96},{64,0},{96,32},{1,65},{33,97},{65,1},{97,33},{2,66}... | collective-permute-start | bytes 786440 | tf_op jit(solution)/shard_map/ppermute | solution.py:427
  7.7 11.9 %collective-permute-start.2 = (bf16[32,4096]{1,0:T(8,128)(2,1)}, bf16[32,4096]{1,0:T(8,128)(2,1)S(1)}, u32[]{:S(2)}, u32[]{:S(2)}) collective-permute-start(bf16[32,4096]{1,0:T(8,128)(2,1)} %get-tuple-element.40), channel_id=1, source_target_pairs={{0,96},{32,0},{64,32},{96,64},{1,97},{33,1},{65,33},{97,65},{2,98}... | collective-permute-start | bytes 786440 | tf_op jit(solution)/shard_map/ppermute | solution.py:427
  100.1 118.2 %all-to-all-start.2 = ((bf16[32,16,4096]{2,1,0:T(8,128)(2,1)}), bf16[32,16,4096]{2,1,0:T(8,128)(2,1)}, u32[]{:S(2)}, u32[]{:S(2)}) async-start(bf16[32,16,4096]{2,1,0:T(8,128)(2,1)} %bitcast.29), calls=%async_computation.2 | async-start | bytes 8388608 | tf_op jit(solution)/shard_map/all_to_all | solution.py:459
  107.2 50.5 %collective-permute-start.3 = (bf16[16,4096]{1,0:T(8,128)(2,1)}, bf16[16,4096]{1,0:T(8,128)(2,1)S(1)}, u32[]{:S(2)}, u32[]{:S(2)}) collective-permute-start(bf16[16,4096]{1,0:T(8,128)(2,1)} %get-tuple-element.42), channel_id=1, source_target_pairs={{0,2},{1,3},{2,4},{3,5},{4,6},{5,7},{6,0},{7,1},{8,10},{9,11},{10,... | collective-permute-start | bytes 393224 | tf_op jit(solution)/shard_map/ppermute | solution.py:490
  108.8 54.1 %collective-permute-start.4 = (bf16[16,4096]{1,0:T(8,128)(2,1)}, bf16[16,4096]{1,0:T(8,128)(2,1)S(1)}, u32[]{:S(2)}, u32[]{:S(2)}) collective-permute-start(bf16[16,4096]{1,0:T(8,128)(2,1)} %get-tuple-element.43), channel_id=1, source_target_pairs={{0,4},{1,5},{2,6},{3,7},{4,0},{5,1},{6,2},{7,3},{8,12},{9,13},{10,... | collective-permute-start | bytes 393224 | tf_op jit(solution)/shard_map/ppermute | solution.py:490
  111.5 51.7 %collective-permute-start.5 = (bf16[16,4096]{1,0:T(8,128)(2,1)}, bf16[16,4096]{1,0:T(8,128)(2,1)S(1)}, u32[]{:S(2)}, u32[]{:S(2)}) collective-permute-start(bf16[16,4096]{1,0:T(8,128)(2,1)} %get-tuple-element.44), channel_id=1, source_target_pairs={{0,6},{1,7},{2,0},{3,1},{4,2},{5,3},{6,4},{7,5},{8,14},{9,15},{10,... | collective-permute-start | bytes 393224 | tf_op jit(solution)/shard_map/ppermute | solution.py:490
  113.0 52.8 %collective-permute-start.6 = (bf16[16,4096]{1,0:T(8,128)(2,1)}, bf16[16,4096]{1,0:T(8,128)(2,1)S(1)}, u32[]{:S(2)}, u32[]{:S(2)}) collective-permute-start(bf16[16,4096]{1,0:T(8,128)(2,1)} %get-tuple-element.45), channel_id=1, source_target_pairs={{0,8},{1,9},{2,10},{3,11},{4,12},{5,13},{6,14},{7,15},{8,16},{9,17... | collective-permute-start | bytes 393224 | tf_op jit(solution)/shard_map/ppermute | solution.py:490
  114.5 54.6 %collective-permute-start.7 = (bf16[16,4096]{1,0:T(8,128)(2,1)}, bf16[16,4096]{1,0:T(8,128)(2,1)S(1)}, u32[]{:S(2)}, u32[]{:S(2)}) collective-permute-start(bf16[16,4096]{1,0:T(8,128)(2,1)} %get-tuple-element.46), channel_id=1, source_target_pairs={{0,10},{1,11},{2,12},{3,13},{4,14},{5,15},{6,8},{7,9},{8,18},{9,19... | collective-permute-start | bytes 393224 | tf_op jit(solution)/shard_map/ppermute | solution.py:490
  157.6 15.8 %collective-permute-start.8 = (bf16[16,4096]{1,0:T(8,128)(2,1)}, bf16[16,4096]{1,0:T(8,128)(2,1)S(1)}, u32[]{:S(2)}, u32[]{:S(2)}) collective-permute-start(bf16[16,4096]{1,0:T(8,128)(2,1)} %get-tuple-element.47), channel_id=1, source_target_pairs={{0,12},{1,13},{2,14},{3,15},{4,8},{5,9},{6,10},{7,11},{8,20},{9,21... | collective-permute-start | bytes 393224 | tf_op jit(solution)/shard_map/ppermute | solution.py:490
  162.9 11.2 %collective-permute-start.9 = (bf16[16,4096]{1,0:T(8,128)(2,1)}, bf16[16,4096]{1,0:T(8,128)(2,1)S(1)}, u32[]{:S(2)}, u32[]{:S(2)}) collective-permute-start(bf16[16,4096]{1,0:T(8,128)(2,1)} %get-tuple-element.48), channel_id=1, source_target_pairs={{0,14},{1,15},{2,8},{3,9},{4,10},{5,11},{6,12},{7,13},{8,22},{9,23... | collective-permute-start | bytes 393224 | tf_op jit(solution)/shard_map/ppermute | solution.py:490
  163.2 19.9 %collective-permute-start.10 = (bf16[16,4096]{1,0:T(8,128)(2,1)}, bf16[16,4096]{1,0:T(8,128)(2,1)S(1)}, u32[]{:S(2)}, u32[]{:S(2)}) collective-permute-start(bf16[16,4096]{1,0:T(8,128)(2,1)} %get-tuple-element.49), channel_id=1, source_target_pairs={{0,16},{1,17},{2,18},{3,19},{4,20},{5,21},{6,22},{7,23},{8,24},{9,... | collective-permute-start | bytes 393224 | tf_op jit(solution)/shard_map/ppermute | solution.py:490
  165.8 17.4 %collective-permute-start.11 = (bf16[16,4096]{1,0:T(8,128)(2,1)}, bf16[16,4096]{1,0:T(8,128)(2,1)S(1)}, u32[]{:S(2)}, u32[]{:S(2)}) collective-permute-start(bf16[16,4096]{1,0:T(8,128)(2,1)} %get-tuple-element.50), channel_id=1, source_target_pairs={{0,18},{1,19},{2,20},{3,21},{4,22},{5,23},{6,16},{7,17},{8,26},{9,... | collective-permute-start | bytes 393224 | tf_op jit(solution)/shard_map/ppermute | solution.py:490
  169.1 17.6 %collective-permute-start.12 = (bf16[16,4096]{1,0:T(8,128)(2,1)}, bf16[16,4096]{1,0:T(8,128)(2,1)S(1)}, u32[]{:S(2)}, u32[]{:S(2)}) collective-permute-start(bf16[16,4096]{1,0:T(8,128)(2,1)} %get-tuple-element.51), channel_id=1, source_target_pairs={{0,20},{1,21},{2,22},{3,23},{4,16},{5,17},{6,18},{7,19},{8,28},{9,... | collective-permute-start | bytes 393224 | tf_op jit(solution)/shard_map/ppermute | solution.py:490
  173.5 14.3 %collective-permute-start.13 = (bf16[16,4096]{1,0:T(8,128)(2,1)}, bf16[16,4096]{1,0:T(8,128)(2,1)S(1)}, u32[]{:S(2)}, u32[]{:S(2)}) collective-permute-start(bf16[16,4096]{1,0:T(8,128)(2,1)} %get-tuple-element.52), channel_id=1, source_target_pairs={{0,22},{1,23},{2,16},{3,17},{4,18},{5,19},{6,20},{7,21},{8,30},{9,... | collective-permute-start | bytes 393224 | tf_op jit(solution)/shard_map/ppermute | solution.py:490
  174.1 13.6 %collective-permute-start.14 = (bf16[16,4096]{1,0:T(8,128)(2,1)}, bf16[16,4096]{1,0:T(8,128)(2,1)S(1)}, u32[]{:S(2)}, u32[]{:S(2)}) collective-permute-start(bf16[16,4096]{1,0:T(8,128)(2,1)} %get-tuple-element.53), channel_id=1, source_target_pairs={{0,24},{1,25},{2,26},{3,27},{4,28},{5,29},{6,30},{7,31},{8,0},{9,1... | collective-permute-start | bytes 393224 | tf_op jit(solution)/shard_map/ppermute | solution.py:490
  183.1 8.2 %collective-permute-start.15 = (bf16[16,4096]{1,0:T(8,128)(2,1)}, bf16[16,4096]{1,0:T(8,128)(2,1)S(1)}, u32[]{:S(2)}, u32[]{:S(2)}) collective-permute-start(bf16[16,4096]{1,0:T(8,128)(2,1)} %get-tuple-element.54), channel_id=1, source_target_pairs={{0,26},{1,27},{2,28},{3,29},{4,30},{5,31},{6,24},{7,25},{8,2},{9,3... | collective-permute-start | bytes 393224 | tf_op jit(solution)/shard_map/ppermute | solution.py:490
  183.2 12.5 %collective-permute-start.16 = (bf16[16,4096]{1,0:T(8,128)(2,1)}, bf16[16,4096]{1,0:T(8,128)(2,1)S(1)}, u32[]{:S(2)}, u32[]{:S(2)}) collective-permute-start(bf16[16,4096]{1,0:T(8,128)(2,1)} %get-tuple-element.55), channel_id=1, source_target_pairs={{0,28},{1,29},{2,30},{3,31},{4,24},{5,25},{6,26},{7,27},{8,4},{9,5... | collective-permute-start | bytes 393224 | tf_op jit(solution)/shard_map/ppermute | solution.py:490
  186.7 9.3 %collective-permute-start.17 = (bf16[16,4096]{1,0:T(8,128)(2,1)}, bf16[16,4096]{1,0:T(8,128)(2,1)S(1)}, u32[]{:S(2)}, u32[]{:S(2)}) collective-permute-start(bf16[16,4096]{1,0:T(8,128)(2,1)} %get-tuple-element.56), channel_id=1, source_target_pairs={{0,30},{1,31},{2,24},{3,25},{4,26},{5,27},{6,28},{7,29},{8,6},{9,7... | collective-permute-start | bytes 393224 | tf_op jit(solution)/shard_map/ppermute | solution.py:490
  199.1 3.0 %collective-permute-start.18 = (bf16[128,4096]{1,0:T(8,128)(2,1)}, bf16[128,4096]{1,0:T(8,128)(2,1)S(1)}, u32[]{:S(2)}, u32[]{:S(2)}) collective-permute-start(bf16[128,4096]{1,0:T(8,128)(2,1)} %shard_map.85), channel_id=1, source_target_pairs={{0,1},{1,0},{2,3},{3,2},{4,5},{5,4},{6,7},{7,6},{8,9},{9,8},{10,11... | collective-permute-start | bytes 3145736 | tf_op jit(solution)/shard_map/ppermute | solution.py:501
  218.3 35.0 %all-to-all-start = ((bf16[32,8,4096]{2,1,0:T(8,128)(2,1)}), bf16[32,8,4096]{2,1,0:T(8,128)(2,1)}, u32[]{:S(2)}, u32[]{:S(2)}) async-start(bf16[32,8,4096]{2,1,0:T(8,128)(2,1)} %shard_map.86), calls=%async_computation | async-start | bytes 4194304 | tf_op jit(solution)/shard_map/all_to_all | solution.py:459
  256.5 12.9 %collective-permute-start.19 = (bf16[32,4096]{1,0:T(8,128)(2,1)}, bf16[32,4096]{1,0:T(8,128)(2,1)S(1)}, u32[]{:S(2)}, u32[]{:S(2)}) collective-permute-start(bf16[32,4096]{1,0:T(8,128)(2,1)} %get-tuple-element.60), channel_id=1, source_target_pairs={{0,96},{32,0},{64,32},{96,64},{1,97},{33,1},{65,33},{97,65},{2,98}... | collective-permute-start | bytes 786440 | tf_op jit(solution)/shard_map/ppermute | solution.py:427
  258.8 10.9 %collective-permute-start.20 = (bf16[32,4096]{1,0:T(8,128)(2,1)}, bf16[32,4096]{1,0:T(8,128)(2,1)S(1)}, u32[]{:S(2)}, u32[]{:S(2)}) collective-permute-start(bf16[32,4096]{1,0:T(8,128)(2,1)} %get-tuple-element.61), channel_id=1, source_target_pairs={{0,64},{32,96},{64,0},{96,32},{1,65},{33,97},{65,1},{97,33},{2,66}... | collective-permute-start | bytes 786440 | tf_op jit(solution)/shard_map/ppermute | solution.py:427
  259.9 13.0 %collective-permute-start.21 = (bf16[32,4096]{1,0:T(8,128)(2,1)}, bf16[32,4096]{1,0:T(8,128)(2,1)S(1)}, u32[]{:S(2)}, u32[]{:S(2)}) collective-permute-start(bf16[32,4096]{1,0:T(8,128)(2,1)} %get-tuple-element.62), channel_id=1, source_target_pairs={{0,32},{32,64},{64,96},{96,0},{1,33},{33,65},{65,97},{97,1},{2,34}... | collective-permute-start | bytes 786440 | tf_op jit(solution)/shard_map/ppermute | solution.py:427
  (19 other events, 288.9 us)

commit v2 on v1

--- a/solution.py
+++ b/solution.py
@@ -332,26 +332,20 @@
         copy.wait()
 
 
-def with_part(res_ref, part_ref, res, part, in_sems, part_sems):
-    cols = parts(res.shape[1], PIECES)
-    loads = [send(part_ref.at[:, c], part.at[:, c], part_sems, j) for j, c in enumerate(cols)]
-    for load in loads:
-        load.start()
-    for j, c in each_piece(res_ref, res, in_sems):
-        loads[j].wait()
-        yield j, c
-
-
-def combine_own_kernel(w_ref, res_ref, part_ref, out_ref, res, part, in_sems, part_sems):
-    for _, c in with_part(res_ref, part_ref, res, part, in_sems, part_sems):
-        out_ref[:, c] = part[:, c] + weighted(w_ref, res[:, c])
+def with_part(part_ref, part, part_sems):
+    return each_piece(part_ref, part, part_sems)
+
+
+def combine_own_kernel(w_ref, res_ref, part_ref, out_ref, part, part_sems):
+    for _, c in with_part(part_ref, part, part_sems):
+        out_ref[:, c] = part[:, c] + weighted(w_ref, res_ref[:, c])
 
 
 def combine_arrived_kernel(room, w_ref, res_ref, part_ref, *refs):
-    *out_refs, res, part, buf, in_sems, part_sems, sems = refs
+    *out_refs, part, buf, part_sems, sems = refs
     copies = []
-    for j, c in with_part(res_ref, part_ref, res, part, in_sems, part_sems):
-        buf[:, c] = (part[:, c] + weighted(w_ref, res[:, c])).astype(BF16)
+    for j, c in with_part(part_ref, part, part_sems):
+        buf[:, c] = (part[:, c] + weighted(w_ref, res_ref[:, c])).astype(BF16)
         for k, out_ref in enumerate(out_refs):
             copies.append(send(buf.at[pl.ds(k * room, room), c], out_ref.at[:, c], sems, j * len(out_refs) + k))
             copies[-1].start()
@@ -546,17 +540,14 @@
         4 * source_rows * cut * width,
         2 * cut * width + 4 * source_rows * width,
     )(own_w[:, :cut], arr_w[:, :cut], in_hbm(back0))
-    back1 = in_hbm(back1)
     arrived_parts = call(
         functools.partial(combine_arrived_kernel, room),
-        [VM, HB, HB],
+        [VM, VM, HB],
         [HB] * peers,
         [hbm((room, width), BF16)] * peers,
         [
-            vmem((rest, width), BF16),
             vmem((moved, width), F32),
             vmem((moved, width), BF16),
-            DMA((PIECES,)),
             DMA((PIECES,)),
             DMA((PIECES * peers,)),
         ],
@@ -566,10 +557,10 @@
     returned = shift(arrived_parts, -1)
     own_part = call(
         combine_own_kernel,
-        [VM, HB, HB],
+        [VM, VM, HB],
         VM,
         vmem((own_rows, width), F32),
-        [vmem((rest, width), BF16), vmem((own_rows, width), F32), DMA((PIECES,)), DMA((PIECES,))],
+        [vmem((own_rows, width), F32), DMA((PIECES,))],
         4 * own_rows * rest * width,
         2 * rest * width + 8 * own_rows * width,
     )(own_w[:, cut:], back1, in_hbm(part_own))

time: 276 us -> 275 us (level)
  no operation moved by 1% of the time
where the time goes in v2:
time: 275 us; the launch traced here: 274 us
  waiting for transfers between devices  105 us (38%)
  blocking collectives  59.4 us (22%)
  Pallas kernels  57.8 us (21%)
  starting transfers between devices  46.9 us (17%)
  local copies, waits for them, and re-layouts  3.02 us (1%)
    ppermute x15, waiting for transfers between devices, local(): landed[j] = in_hbm(lax.ppermute(blocks[j], 'expert', pairs))  61.7 us
    all_to_all x1, blocking collectives, exchange(): lax.all_to_all(shaped, 'expert', split_axis=0, concat_axis=0, tiled=True)  59.4 us
    pallas_call x2, Pallas kernels, experts(): call(functools.partial(ffn_kernel, blocks, len(inputs)), [SM] + [HB] * (l...  33.9 us
    ppermute x15, starting transfers between devices, local(): landed[j] = in_hbm(lax.ppermute(blocks[j], 'expert', pairs))  27.1 us
    all_to_all x2, waiting for transfers between devices, exchange(): lax.all_to_all(shaped, 'expert', split_axis=0, concat_axis=0, tiled=True)  25.3 us
    ppermute x6, waiting for transfers between devices, shift(): sent[k] = lax.ppermute(blocks[k - 1], 'dp', pairs)  15.4 us
    ppermute x6, starting transfers between devices, shift(): sent[k] = lax.ppermute(blocks[k - 1], 'dp', pairs)  9.97 us
    all_to_all x2, starting transfers between devices, exchange(): lax.all_to_all(shaped, 'expert', split_axis=0, concat_axis=0, tiled=True)  9.72 us
  transfers between devices with their start and end apart: 24, of which 13 were waited for; matrix products, arithmetic and copies ran while one was open for 0% of the time, Pallas kernels for 11%

profile of v2, /device:TPU:0, one launch (start us, length us, event | category | flops | bytes accessed | tf_op | source)
XLA Modules:
  0.0 273.9 jit_solution(14392130954703398337)
XLA Ops:
  0.1 3.2 %shard_map.82 = (bf16[96,128]{1,0:T(8,128)(2,1)S(1)}, bf16[128,4096]{1,0:T(8,128)(2,1)S(1)}, bf16[32,4096]{1,0:T(8,128)(2,1)}, bf16[32,4096]{1,0:T(8,128)(2,1)}, bf16[32,4096]{1,0:T(8,128)(2,1)}) custom-call(s32[2]{0:T(128)S(1)} %pad_add_fusion.me_ref, s32[4,128]{1,0:T(4,128)} %bitcast.21, bf16[128,4096]{1,0:T(8,128)(2,1)} %bitcast.33), custom_call_target="tpu_custom_call" | custom-call | flops 100663296 | bytes 2097152 | tf_op jit(solution)/shard_map/pallas_call | solution.py:424
  5.0 2.7 collective-permute-start.1
  14.1 5.4 %collective-permute-done.1.refs_2_ = bf16[32,4096]{1,0:T(8,128)(2,1)S(1)} collective-permute-done((bf16[32,4096]{1,0:T(8,128)(2,1)}, bf16[32,4096]{1,0:T(8,128)(2,1)S(1)}, u32[]{:S(2)}, u32[]{:S(2)}) %collective-permute-start.1) | collective-permute-done | bytes 262176 | tf_op jit(solution)/shard_map/ppermute | solution.py:421
  19.6 2.5 shard_map.87
  22.1 59.4 %all_to_all.15 = bf16[32,16,4096]{2,1,0:T(8,128)(2,1)} all-to-all(bf16[32,16,4096]{2,1,0:T(8,128)(2,1)} %bitcast.24), channel_id=1, replica_groups=mesh['dp'=4,'expert'=32] {'expert'}, dimensions={0} | all-to-all | bytes 8388608 | tf_op jit(solution)/shard_map/all_to_all | solution.py:453
  81.5 18.6 %shard_map.88 = bf16[512,4096]{1,0:T(8,128)(2,1)} custom-call(s32[2]{0:T(128)} %copy-done, bf16[512,4096]{1,0:T(8,128)(2,1)} %bitcast.32, bf16[4096,896]{1,0:T(8,128)(2,1)} %bitcast.25, bf16[4096,896]{1,0:T(8,128)(2,1)} %bitcast.27, bf16[896,4096]{1,0:T(8,128)(2,1)} %bitcast.29), custom_call_target="tpu_custom_call" | custom-call | flops 11274289152 | bytes 30408704 | tf_op jit(solution)/shard_map/pallas_call | solution.py:501
  100.1 4.9 %all-to-all-start.2 = ((bf16[32,16,4096]{2,1,0:T(8,128)(2,1)}), bf16[32,16,4096]{2,1,0:T(8,128)(2,1)}, u32[]{:S(2)}, u32[]{:S(2)}) async-start(bf16[32,16,4096]{2,1,0:T(8,128)(2,1)} %bitcast.31), calls=%async_computation.2 | async-start | bytes 8388608 | tf_op jit(solution)/shard_map/all_to_all | solution.py:453
  108.8 2.7 collective-permute-start.4
  116.0 41.6 %collective-permute-done.3.refs_1_ = bf16[16,4096]{1,0:T(8,128)(2,1)S(1)} collective-permute-done((bf16[16,4096]{1,0:T(8,128)(2,1)}, bf16[16,4096]{1,0:T(8,128)(2,1)S(1)}, u32[]{:S(2)}, u32[]{:S(2)}) %collective-permute-start.3) | collective-permute-done | bytes 131104 | tf_op jit(solution)/shard_map/ppermute | solution.py:484
  157.6 3.3 %collective-permute-start.8 = (bf16[16,4096]{1,0:T(8,128)(2,1)}, bf16[16,4096]{1,0:T(8,128)(2,1)S(1)}, u32[]{:S(2)}, u32[]{:S(2)}) collective-permute-start(bf16[16,4096]{1,0:T(8,128)(2,1)} %get-tuple-element.47), channel_id=1, source_target_pairs={{0,12},{1,13},{2,14},{3,15},{4,8},{5,9},{6,10},{7,11},{8,20},{9,21... | collective-permute-start | bytes 393224 | tf_op jit(solution)/shard_map/ppermute | solution.py:484
  163.2 2.6 collective-permute-start.10
  165.8 3.3 %collective-permute-start.11 = (bf16[16,4096]{1,0:T(8,128)(2,1)}, bf16[16,4096]{1,0:T(8,128)(2,1)S(1)}, u32[]{:S(2)}, u32[]{:S(2)}) collective-permute-start(bf16[16,4096]{1,0:T(8,128)(2,1)} %get-tuple-element.50), channel_id=1, source_target_pairs={{0,18},{1,19},{2,20},{3,21},{4,22},{5,23},{6,16},{7,17},{8,26},{9,... | collective-permute-start | bytes 393224 | tf_op jit(solution)/shard_map/ppermute | solution.py:484
  175.5 7.6 %collective-permute-done.10.refs_8_ = bf16[16,4096]{1,0:T(8,128)(2,1)S(1)} collective-permute-done((bf16[16,4096]{1,0:T(8,128)(2,1)}, bf16[16,4096]{1,0:T(8,128)(2,1)S(1)}, u32[]{:S(2)}, u32[]{:S(2)}) %collective-permute-start.10) | collective-permute-done | bytes 131104 | tf_op jit(solution)/shard_map/ppermute | solution.py:484
  183.2 3.6 %collective-permute-start.16 = (bf16[16,4096]{1,0:T(8,128)(2,1)}, bf16[16,4096]{1,0:T(8,128)(2,1)S(1)}, u32[]{:S(2)}, u32[]{:S(2)}) collective-permute-start(bf16[16,4096]{1,0:T(8,128)(2,1)} %get-tuple-element.55), channel_id=1, source_target_pairs={{0,28},{1,29},{2,30},{3,31},{4,24},{5,25},{6,26},{7,27},{8,4},{9,5... | collective-permute-start | bytes 393224 | tf_op jit(solution)/shard_map/ppermute | solution.py:484
  187.8 3.6 %collective-permute-done.15.refs_13_ = bf16[16,4096]{1,0:T(8,128)(2,1)S(1)} collective-permute-done((bf16[16,4096]{1,0:T(8,128)(2,1)}, bf16[16,4096]{1,0:T(8,128)(2,1)S(1)}, u32[]{:S(2)}, u32[]{:S(2)}) %collective-permute-start.15) | collective-permute-done | bytes 131104 | tf_op jit(solution)/shard_map/ppermute | solution.py:484
  191.4 4.2 %collective-permute-done.16.refs_14_ = bf16[16,4096]{1,0:T(8,128)(2,1)S(1)} collective-permute-done((bf16[16,4096]{1,0:T(8,128)(2,1)}, bf16[16,4096]{1,0:T(8,128)(2,1)S(1)}, u32[]{:S(2)}, u32[]{:S(2)}) %collective-permute-start.16) | collective-permute-done | bytes 131104 | tf_op jit(solution)/shard_map/ppermute | solution.py:484
  199.2 2.9 %collective-permute-done.18.refs_16_ = bf16[128,4096]{1,0:T(8,128)(2,1)S(1)} collective-permute-done((bf16[128,4096]{1,0:T(8,128)(2,1)}, bf16[128,4096]{1,0:T(8,128)(2,1)S(1)}, u32[]{:S(2)}, u32[]{:S(2)}) %collective-permute-start.18) | collective-permute-done | bytes 1048608 | tf_op jit(solution)/shard_map/ppermute | solution.py:495
  203.0 15.3 %shard_map.86 = bf16[32,8,4096]{2,1,0:T(8,128)(2,1)} custom-call(s32[2]{0:T(128)} %copy-done, bf16[16,4096]{1,0:T(8,128)(2,1)} %get-tuple-element.41.refs_0_, bf16[16,4096]{1,0:T(8,128)(2,1)} %copy-done.4, bf16[16,4096]{1,0:T(8,128)(2,1)} %copy-done.5, bf16[16,4096]{1,0:T(8,128)(2,1)} %copy-done.6, bf16[16,4096]{1,0:T(8,128)(2,1)} %copy-done.7, ...), custom_call_target="tpu_custom_call" | custom-call | flops 5637144576 | bytes 26214400 | tf_op jit(solution)/shard_map/pallas_call | solution.py:501
  218.3 4.9 %all-to-all-start = ((bf16[32,8,4096]{2,1,0:T(8,128)(2,1)}), bf16[32,8,4096]{2,1,0:T(8,128)(2,1)S(1)}, u32[]{:S(2)}, u32[]{:S(2)}) async-start(bf16[32,8,4096]{2,1,0:T(8,128)(2,1)} %shard_map.86), calls=%async_computation | async-start | bytes 4194304 | tf_op jit(solution)/shard_map/all_to_all | solution.py:453
  223.2 4.7 %shard_map.89 = (f32[128,4096]{1,0:T(8,128)}, f32[96,4096]{1,0:T(8,128)}) custom-call(bf16[256,512]{1,0:T(8,128)(2,1)S(1)} %slice.20.own_w_ref, bf16[192,512]{1,0:T(8,128)(2,1)S(1)} %slice.21.arr_w_ref, bf16[512,4096]{1,0:T(8,128)(2,1)} %bitcast.15.res_ref), custom_call_target="tpu_custom_call" | custom-call | flops 1879048192 | bytes 7864320 | tf_op jit(solution)/shard_map/pallas_call | solution.py:528
  228.0 25.3 %all-to-all-done = bf16[32,8,4096]{2,1,0:T(8,128)(2,1)S(1)} async-done(((bf16[32,8,4096]{2,1,0:T(8,128)(2,1)}), bf16[32,8,4096]{2,1,0:T(8,128)(2,1)S(1)}, u32[]{:S(2)}, u32[]{:S(2)}) %all-to-all-start) | async-done | bytes 2097184 | tf_op jit(solution)/shard_map/all_to_all | solution.py:453
  253.2 2.9 %shard_map.91 = (bf16[32,4096]{1,0:T(8,128)(2,1)}, bf16[32,4096]{1,0:T(8,128)(2,1)}, bf16[32,4096]{1,0:T(8,128)(2,1)}) custom-call(bf16[192,256]{1,0:T(8,128)(2,1)S(1)} %slice.23.w_ref, bf16[256,4096]{1,0:T(8,128)(2,1)S(1)} %bitcast.19, f32[96,4096]{1,0:T(8,128)} %get-tuple-element.59.part_ref), custom_call_target="tpu_custom_call" | custom-call | flops 402653184 | bytes 4456448 | tf_op jit(solution)/shard_map/pallas_call | solution.py:543
  262.6 6.4 %collective-permute-done.19.refs_0_ = bf16[32,4096]{1,0:T(8,128)(2,1)S(1)} collective-permute-done((bf16[32,4096]{1,0:T(8,128)(2,1)}, bf16[32,4096]{1,0:T(8,128)(2,1)S(1)}, u32[]{:S(2)}, u32[]{:S(2)}) %collective-permute-start.19) | collective-permute-done | bytes 262176 | tf_op jit(solution)/shard_map/ppermute | solution.py:421
  269.4 3.2 %collective-permute-done.21.refs_2_ = bf16[32,4096]{1,0:T(8,128)(2,1)S(1)} collective-permute-done((bf16[32,4096]{1,0:T(8,128)(2,1)}, bf16[32,4096]{1,0:T(8,128)(2,1)S(1)}, u32[]{:S(2)}, u32[]{:S(2)}) %collective-permute-start.21) | collective-permute-done | bytes 262176 | tf_op jit(solution)/shard_map/ppermute | solution.py:421
  (83 shorter events, 38.7 us)
Async XLA Ops:
  3.3 10.8 %collective-permute-start = (bf16[32,4096]{1,0:T(8,128)(2,1)}, bf16[32,4096]{1,0:T(8,128)(2,1)S(1)}, u32[]{:S(2)}, u32[]{:S(2)}) collective-permute-start(bf16[32,4096]{1,0:T(8,128)(2,1)} %get-tuple-element.38), channel_id=1, source_target_pairs={{0,32},{32,64},{64,96},{96,0},{1,33},{33,65},{65,97},{97,1},{2,34}... | collective-permute-start | bytes 786440 | tf_op jit(solution)/shard_map/ppermute | solution.py:421
  5.0 14.6 %collective-permute-start.1 = (bf16[32,4096]{1,0:T(8,128)(2,1)}, bf16[32,4096]{1,0:T(8,128)(2,1)S(1)}, u32[]{:S(2)}, u32[]{:S(2)}) collective-permute-start(bf16[32,4096]{1,0:T(8,128)(2,1)} %get-tuple-element.39), channel_id=1, source_target_pairs={{0,64},{32,96},{64,0},{96,32},{1,65},{33,97},{65,1},{97,33},{2,66}... | collective-permute-start | bytes 786440 | tf_op jit(solution)/shard_map/ppermute | solution.py:421
  7.7 11.9 %collective-permute-start.2 = (bf16[32,4096]{1,0:T(8,128)(2,1)}, bf16[32,4096]{1,0:T(8,128)(2,1)S(1)}, u32[]{:S(2)}, u32[]{:S(2)}) collective-permute-start(bf16[32,4096]{1,0:T(8,128)(2,1)} %get-tuple-element.40), channel_id=1, source_target_pairs={{0,96},{32,0},{64,32},{96,64},{1,97},{33,1},{65,33},{97,65},{2,98}... | collective-permute-start | bytes 786440 | tf_op jit(solution)/shard_map/ppermute | solution.py:421
  100.1 118.2 %all-to-all-start.2 = ((bf16[32,16,4096]{2,1,0:T(8,128)(2,1)}), bf16[32,16,4096]{2,1,0:T(8,128)(2,1)}, u32[]{:S(2)}, u32[]{:S(2)}) async-start(bf16[32,16,4096]{2,1,0:T(8,128)(2,1)} %bitcast.31), calls=%async_computation.2 | async-start | bytes 8388608 | tf_op jit(solution)/shard_map/all_to_all | solution.py:453
  107.2 50.5 %collective-permute-start.3 = (bf16[16,4096]{1,0:T(8,128)(2,1)}, bf16[16,4096]{1,0:T(8,128)(2,1)S(1)}, u32[]{:S(2)}, u32[]{:S(2)}) collective-permute-start(bf16[16,4096]{1,0:T(8,128)(2,1)} %get-tuple-element.42), channel_id=1, source_target_pairs={{0,2},{1,3},{2,4},{3,5},{4,6},{5,7},{6,0},{7,1},{8,10},{9,11},{10,... | collective-permute-start | bytes 393224 | tf_op jit(solution)/shard_map/ppermute | solution.py:484
  108.8 54.1 %collective-permute-start.4 = (bf16[16,4096]{1,0:T(8,128)(2,1)}, bf16[16,4096]{1,0:T(8,128)(2,1)S(1)}, u32[]{:S(2)}, u32[]{:S(2)}) collective-permute-start(bf16[16,4096]{1,0:T(8,128)(2,1)} %get-tuple-element.43), channel_id=1, source_target_pairs={{0,4},{1,5},{2,6},{3,7},{4,0},{5,1},{6,2},{7,3},{8,12},{9,13},{10,... | collective-permute-start | bytes 393224 | tf_op jit(solution)/shard_map/ppermute | solution.py:484
  111.5 51.7 %collective-permute-start.5 = (bf16[16,4096]{1,0:T(8,128)(2,1)}, bf16[16,4096]{1,0:T(8,128)(2,1)S(1)}, u32[]{:S(2)}, u32[]{:S(2)}) collective-permute-start(bf16[16,4096]{1,0:T(8,128)(2,1)} %get-tuple-element.44), channel_id=1, source_target_pairs={{0,6},{1,7},{2,0},{3,1},{4,2},{5,3},{6,4},{7,5},{8,14},{9,15},{10,... | collective-permute-start | bytes 393224 | tf_op jit(solution)/shard_map/ppermute | solution.py:484
  113.0 52.8 %collective-permute-start.6 = (bf16[16,4096]{1,0:T(8,128)(2,1)}, bf16[16,4096]{1,0:T(8,128)(2,1)S(1)}, u32[]{:S(2)}, u32[]{:S(2)}) collective-permute-start(bf16[16,4096]{1,0:T(8,128)(2,1)} %get-tuple-element.45), channel_id=1, source_target_pairs={{0,8},{1,9},{2,10},{3,11},{4,12},{5,13},{6,14},{7,15},{8,16},{9,17... | collective-permute-start | bytes 393224 | tf_op jit(solution)/shard_map/ppermute | solution.py:484
  114.5 54.6 %collective-permute-start.7 = (bf16[16,4096]{1,0:T(8,128)(2,1)}, bf16[16,4096]{1,0:T(8,128)(2,1)S(1)}, u32[]{:S(2)}, u32[]{:S(2)}) collective-permute-start(bf16[16,4096]{1,0:T(8,128)(2,1)} %get-tuple-element.46), channel_id=1, source_target_pairs={{0,10},{1,11},{2,12},{3,13},{4,14},{5,15},{6,8},{7,9},{8,18},{9,19... | collective-permute-start | bytes 393224 | tf_op jit(solution)/shard_map/ppermute | solution.py:484
  157.6 15.8 %collective-permute-start.8 = (bf16[16,4096]{1,0:T(8,128)(2,1)}, bf16[16,4096]{1,0:T(8,128)(2,1)S(1)}, u32[]{:S(2)}, u32[]{:S(2)}) collective-permute-start(bf16[16,4096]{1,0:T(8,128)(2,1)} %get-tuple-element.47), channel_id=1, source_target_pairs={{0,12},{1,13},{2,14},{3,15},{4,8},{5,9},{6,10},{7,11},{8,20},{9,21... | collective-permute-start | bytes 393224 | tf_op jit(solution)/shard_map/ppermute | solution.py:484
  162.9 11.2 %collective-permute-start.9 = (bf16[16,4096]{1,0:T(8,128)(2,1)}, bf16[16,4096]{1,0:T(8,128)(2,1)S(1)}, u32[]{:S(2)}, u32[]{:S(2)}) collective-permute-start(bf16[16,4096]{1,0:T(8,128)(2,1)} %get-tuple-element.48), channel_id=1, source_target_pairs={{0,14},{1,15},{2,8},{3,9},{4,10},{5,11},{6,12},{7,13},{8,22},{9,23... | collective-permute-start | bytes 393224 | tf_op jit(solution)/shard_map/ppermute | solution.py:484
  163.2 19.9 %collective-permute-start.10 = (bf16[16,4096]{1,0:T(8,128)(2,1)}, bf16[16,4096]{1,0:T(8,128)(2,1)S(1)}, u32[]{:S(2)}, u32[]{:S(2)}) collective-permute-start(bf16[16,4096]{1,0:T(8,128)(2,1)} %get-tuple-element.49), channel_id=1, source_target_pairs={{0,16},{1,17},{2,18},{3,19},{4,20},{5,21},{6,22},{7,23},{8,24},{9,... | collective-permute-start | bytes 393224 | tf_op jit(solution)/shard_map/ppermute | solution.py:484
  165.8 17.4 %collective-permute-start.11 = (bf16[16,4096]{1,0:T(8,128)(2,1)}, bf16[16,4096]{1,0:T(8,128)(2,1)S(1)}, u32[]{:S(2)}, u32[]{:S(2)}) collective-permute-start(bf16[16,4096]{1,0:T(8,128)(2,1)} %get-tuple-element.50), channel_id=1, source_target_pairs={{0,18},{1,19},{2,20},{3,21},{4,22},{5,23},{6,16},{7,17},{8,26},{9,... | collective-permute-start | bytes 393224 | tf_op jit(solution)/shard_map/ppermute | solution.py:484
  169.1 17.6 %collective-permute-start.12 = (bf16[16,4096]{1,0:T(8,128)(2,1)}, bf16[16,4096]{1,0:T(8,128)(2,1)S(1)}, u32[]{:S(2)}, u32[]{:S(2)}) collective-permute-start(bf16[16,4096]{1,0:T(8,128)(2,1)} %get-tuple-element.51), channel_id=1, source_target_pairs={{0,20},{1,21},{2,22},{3,23},{4,16},{5,17},{6,18},{7,19},{8,28},{9,... | collective-permute-start | bytes 393224 | tf_op jit(solution)/shard_map/ppermute | solution.py:484
  173.5 14.3 %collective-permute-start.13 = (bf16[16,4096]{1,0:T(8,128)(2,1)}, bf16[16,4096]{1,0:T(8,128)(2,1)S(1)}, u32[]{:S(2)}, u32[]{:S(2)}) collective-permute-start(bf16[16,4096]{1,0:T(8,128)(2,1)} %get-tuple-element.52), channel_id=1, source_target_pairs={{0,22},{1,23},{2,16},{3,17},{4,18},{5,19},{6,20},{7,21},{8,30},{9,... | collective-permute-start | bytes 393224 | tf_op jit(solution)/shard_map/ppermute | solution.py:484
  174.1 13.6 %collective-permute-start.14 = (bf16[16,4096]{1,0:T(8,128)(2,1)}, bf16[16,4096]{1,0:T(8,128)(2,1)S(1)}, u32[]{:S(2)}, u32[]{:S(2)}) collective-permute-start(bf16[16,4096]{1,0:T(8,128)(2,1)} %get-tuple-element.53), channel_id=1, source_target_pairs={{0,24},{1,25},{2,26},{3,27},{4,28},{5,29},{6,30},{7,31},{8,0},{9,1... | collective-permute-start | bytes 393224 | tf_op jit(solution)/shard_map/ppermute | solution.py:484
  183.1 8.2 %collective-permute-start.15 = (bf16[16,4096]{1,0:T(8,128)(2,1)}, bf16[16,4096]{1,0:T(8,128)(2,1)S(1)}, u32[]{:S(2)}, u32[]{:S(2)}) collective-permute-start(bf16[16,4096]{1,0:T(8,128)(2,1)} %get-tuple-element.54), channel_id=1, source_target_pairs={{0,26},{1,27},{2,28},{3,29},{4,30},{5,31},{6,24},{7,25},{8,2},{9,3... | collective-permute-start | bytes 393224 | tf_op jit(solution)/shard_map/ppermute | solution.py:484
  183.2 12.5 %collective-permute-start.16 = (bf16[16,4096]{1,0:T(8,128)(2,1)}, bf16[16,4096]{1,0:T(8,128)(2,1)S(1)}, u32[]{:S(2)}, u32[]{:S(2)}) collective-permute-start(bf16[16,4096]{1,0:T(8,128)(2,1)} %get-tuple-element.55), channel_id=1, source_target_pairs={{0,28},{1,29},{2,30},{3,31},{4,24},{5,25},{6,26},{7,27},{8,4},{9,5... | collective-permute-start | bytes 393224 | tf_op jit(solution)/shard_map/ppermute | solution.py:484
  186.7 9.3 %collective-permute-start.17 = (bf16[16,4096]{1,0:T(8,128)(2,1)}, bf16[16,4096]{1,0:T(8,128)(2,1)S(1)}, u32[]{:S(2)}, u32[]{:S(2)}) collective-permute-start(bf16[16,4096]{1,0:T(8,128)(2,1)} %get-tuple-element.56), channel_id=1, source_target_pairs={{0,30},{1,31},{2,24},{3,25},{4,26},{5,27},{6,28},{7,29},{8,6},{9,7... | collective-permute-start | bytes 393224 | tf_op jit(solution)/shard_map/ppermute | solution.py:484
  199.1 3.0 %collective-permute-start.18 = (bf16[128,4096]{1,0:T(8,128)(2,1)}, bf16[128,4096]{1,0:T(8,128)(2,1)S(1)}, u32[]{:S(2)}, u32[]{:S(2)}) collective-permute-start(bf16[128,4096]{1,0:T(8,128)(2,1)} %shard_map.85), channel_id=1, source_target_pairs={{0,1},{1,0},{2,3},{3,2},{4,5},{5,4},{6,7},{7,6},{8,9},{9,8},{10,11... | collective-permute-start | bytes 3145736 | tf_op jit(solution)/shard_map/ppermute | solution.py:495
  218.3 34.9 %all-to-all-start = ((bf16[32,8,4096]{2,1,0:T(8,128)(2,1)}), bf16[32,8,4096]{2,1,0:T(8,128)(2,1)S(1)}, u32[]{:S(2)}, u32[]{:S(2)}) async-start(bf16[32,8,4096]{2,1,0:T(8,128)(2,1)} %shard_map.86), calls=%async_computation | async-start | bytes 4194304 | tf_op jit(solution)/shard_map/all_to_all | solution.py:453
  256.1 12.8 %collective-permute-start.19 = (bf16[32,4096]{1,0:T(8,128)(2,1)}, bf16[32,4096]{1,0:T(8,128)(2,1)S(1)}, u32[]{:S(2)}, u32[]{:S(2)}) collective-permute-start(bf16[32,4096]{1,0:T(8,128)(2,1)} %get-tuple-element.60), channel_id=1, source_target_pairs={{0,96},{32,0},{64,32},{96,64},{1,97},{33,1},{65,33},{97,65},{2,98}... | collective-permute-start | bytes 786440 | tf_op jit(solution)/shard_map/ppermute | solution.py:421
  258.5 10.9 %collective-permute-start.20 = (bf16[32,4096]{1,0:T(8,128)(2,1)}, bf16[32,4096]{1,0:T(8,128)(2,1)S(1)}, u32[]{:S(2)}, u32[]{:S(2)}) collective-permute-start(bf16[32,4096]{1,0:T(8,128)(2,1)} %get-tuple-element.61), channel_id=1, source_target_pairs={{0,64},{32,96},{64,0},{96,32},{1,65},{33,97},{65,1},{97,33},{2,66}... | collective-permute-start | bytes 786440 | tf_op jit(solution)/shard_map/ppermute | solution.py:421
  259.6 12.9 %collective-permute-start.21 = (bf16[32,4096]{1,0:T(8,128)(2,1)}, bf16[32,4096]{1,0:T(8,128)(2,1)S(1)}, u32[]{:S(2)}, u32[]{:S(2)}) collective-permute-start(bf16[32,4096]{1,0:T(8,128)(2,1)} %get-tuple-element.62), channel_id=1, source_target_pairs={{0,32},{32,64},{64,96},{96,0},{1,33},{33,65},{65,97},{97,1},{2,34}... | collective-permute-start | bytes 786440 | tf_op jit(solution)/shard_map/ppermute | solution.py:421
  (19 other events, 288.9 us)
